TPU v7x, 32 devices: a whole 2x2x4 slice. The times are simulated.
32 devices in a mesh: tp: 4 (over z), dp: 8 (over y, x, core).
Axes of the slice: x: 2, y: 2, z: 4, core: 2. Of those that a mesh axis runs over, the one named last changes fastest.
Arguments:
- hidden: bfloat16 [2048, 640], P('dp')
- embedding: bfloat16 [262144, 640], P('tp')
- norm_weight: float32 [640], replicated
- teach_ids: int32 [2048, 256], P('dp')
- teach_prob: float32 [2048, 256], P('dp')
- tok_mask: float32 [2048], P('dp')
Outputs:
- output 1: float32 [], replicated
- output 2: bfloat16 [2048, 640], P('dp')
- output 3: float32 [262144, 640], P('tp', 'dp')
- output 4: float32 [640], replicated
All inputs are finite; a program needn't handle non-finite values.
Results may differ from a plain program's by a relative error of at most 0.001.
Values sent between devices are 32-bit elements.
A program may use at most 1 GiB of HBM per device.

v0:
```python
import jax
import jax.numpy as jnp
from jax import lax
from jax.sharding import PartitionSpec as P

EPS_NORM = 1e-6


def solution(mesh):
    def local_head(hidden, embedding, norm_weight, teach_ids, teach_prob, tok_mask):
        vocab_local = embedding.shape[0]
        tok_local = hidden.shape[0]
        shard_pos = lax.axis_index('tp')
        mask_total = lax.psum(jnp.sum(tok_mask), 'dp')
        scale_w = 1.0 + norm_weight
        h_f32 = hidden.astype(jnp.float32)
        inv_rms = lax.rsqrt(jnp.mean(h_f32 * h_f32, axis=1, keepdims=True) + EPS_NORM)
        normed = h_f32 * inv_rms
        normed_bf = (normed * scale_w).astype(jnp.bfloat16)
        logits = lax.dot_general(normed_bf, embedding, (((1,), (1,)), ((), ())), preferred_element_type=jnp.float32)
        row_max = lax.pmax(jnp.max(logits, axis=1, keepdims=True), 'tp')
        shifted = jnp.exp(logits - row_max)
        local_ids = teach_ids - shard_pos * vocab_local
        in_range = (local_ids >= 0) & (local_ids < vocab_local)
        safe_ids = jnp.where(in_range, local_ids, 0)
        picked = jnp.take_along_axis(logits, safe_ids, axis=1)
        teach_part = jnp.sum(jnp.where(in_range, teach_prob * picked, 0.0), axis=1)
        row_stats = lax.psum(jnp.stack([jnp.sum(shifted, axis=1), teach_part], axis=1), 'tp')
        sum_exp = row_stats[:, 0:1]
        log_norm = row_max + jnp.log(sum_exp)
        loss_sum = lax.psum(jnp.sum(tok_mask * (row_stats[:, 1] - log_norm[:, 0])), 'dp')
        loss_mean = -loss_sum / mask_total
        weight = (tok_mask / mask_total)[:, None]
        soft_prob = shifted * (1.0 / sum_exp)
        row_ids = jnp.arange(tok_local)[:, None]
        d_logits = (soft_prob * weight).at[row_ids, safe_ids].add(jnp.where(in_range, -teach_prob * weight, 0.0))
        dlogit_bf = d_logits.astype(jnp.bfloat16)
        grad_u = lax.psum(jnp.dot(dlogit_bf, embedding, preferred_element_type=jnp.float32), 'tp')
        embed_part = lax.dot_general(dlogit_bf, normed_bf, (((0,), (0,)), ((), ())), preferred_element_type=jnp.float32)
        grad_embed = lax.psum_scatter(embed_part, 'dp', scatter_dimension=1, tiled=True)
        d_normed = grad_u * scale_w
        grad_hidden = (inv_rms * (d_normed - normed * jnp.mean(d_normed * normed, axis=1, keepdims=True))).astype(jnp.bfloat16)
        grad_norm = lax.psum(jnp.sum(grad_u * normed, axis=0), 'dp')
        return loss_mean, grad_hidden, grad_embed, grad_norm

    return jax.shard_map(local_head, mesh=mesh, in_specs=(P('dp', None), P('tp', None), P(None), P('dp', None), P('dp', None), P('dp')), out_specs=(P(), P('dp', None), P('tp', 'dp'), P(None)), check_vma=False)
```

profile of v0, /device:TPU:0, one launch (start us, length us, event | category | flops | bytes accessed | tf_op | source)
XLA Modules:
  0.0 4346.6 jit_solution(6375132756457993394)
XLA Ops:
  8.0 1.1 fusion.11
  9.2 0.7 broadcast_add_fusion
  9.9 1.1 or_bitcast_fusion
  11.0 0.1 copy.10
  11.1 0.8 and_reduce_fusion
  12.0 0.8 multiply_reduce_fusion
  12.8 0.8 copy.12
  13.6 54.9 %fusion.19 = (f32[256]{0:T(256)S(1)}, f32[256,65536]{1,0:T(8,128)}) fusion(bf16[65536,640]{1,0:T(8,128)(2,1)} %param.7, bf16[256,640]{1,0:T(8,128)(2,1)} %param.6, f32[640]{0:T(1024)S(1)} %broadcast_add_fusion, f32[256]{0:T(256)S(1)} %add_rsqrt_fusion), kind=kOutput, calls=%fused_computation.39 | convolution fusion | flops 21492269056 | bytes 151327232 | tf_op jit(solution)/shard_map/dot_general | solution.py:20
  68.5 13.5 pmax.7
  82.0 1572.1 %gather_fusion = f32[65536]{0:T(1024)S(1)} fusion(f32[256,65536]{1,0:T(8,128)} %get-tuple-element.17, s32[65536]{0:T(1024)S(1)} %bitcast.28), kind=kCustom, calls=%fused_computation | custom fusion | bytes 1048576 | tf_op jit(solution)/shard_map/jit(take_along_axis)/gather | solution.py:26
  1654.2 0.1 reshape.43
  1654.3 21.2 fusion
  1675.4 0.2 select_reduce_fusion
  1675.7 989.2 %psum.35 = f32[256,2]{0,1:T(2,128)S(1)} all-reduce(f32[256,2]{0,1:T(2,128)S(1)} %pad_maximum_fusion), channel_id=1, replica_groups=mesh['tp'=4,'dp'=8] {'tp'}, use_global_device_ids=true, to_apply=%region_5.6 | all-reduce | flops 512 | bytes 4096 | tf_op jit(solution)/shard_map/psum | solution.py:28
  2664.9 0.6 fusion.17
  2665.5 12.6 psum.37
  2678.1 0.6 broadcast_divide_fusion
  2678.7 0.1 select_bitcast_fusion.1
  2678.8 43.7 %multiply_bitcast_fusion = f32[32,512,8,128]{3,2,1,0:T(8,128)} fusion(f32[256,65536]{1,0:T(8,128)} %get-tuple-element.17, f32[256]{0:T(256)S(1)} %broadcast_divide_fusion, f32[256]{0:T(256)S(1)} %bitcast.37, f32[256]{0:T(256)S(1)} %bitcast.32), kind=kLoop, calls=%fused_computation.2 | loop fusion | flops 50331648 | bytes 134220800
  2722.6 44.2 %copy.11 = f32[32,512,8,128]{3,1,2,0:T(8,128)} copy(f32[32,512,8,128]{3,2,1,0:T(8,128)} %multiply_bitcast_fusion) | data formatting | bytes 134217728
  2766.8 0.1 copy.13
  2767.0 18.2 sort
  2785.1 462.0 %scatter_fusion = f32[16777216]{0:T(1024)} fusion(f32[16777216]{0:T(1024)} %bitcast.11, s32[65536]{0:T(1024)S(1)} %get-tuple-element.4, f32[65536]{0:T(1024)S(1)} %get-tuple-element.5), kind=kCustom, calls=%fused_computation.1 | custom fusion | flops 65536 | bytes 1048576
  3247.2 32.3 convert_element_type.16
  3279.4 39.5 reshape.39
  3319.0 41.1 fusion.20
  3360.1 0.0 reduce-scatter.2.cloned.1.call-start
  3360.1 67.7 %fusion.13 = f32[65536,640]{0,1:T(8,128)} fusion(bf16[256,65536]{1,0:T(8,128)(2,1)} %reshape.39, bf16[256,640]{1,0:T(8,128)(2,1)S(1)} %copy-done, f32[640]{0:T(1024)S(1)} %copy-done.3, f32[256]{0:T(256)S(1)} %copy-done.5), kind=kOutput, calls=%fused_computation.28 | convolution fusion | flops 21475491840 | bytes 201657856 | tf_op jit(solution)/shard_map/dot_general | solution.py:39
  3427.9 1.4 fusion.10
  3429.3 12.6 all-reduce
  3443.3 2.0 fusion.9
  3445.3 892.8 %reduce-scatter.2.cloned.1.call-done = f32[65536,80]{0,1:T(8,128)} async-done(((f32[65536,640]{0,1:T(8,128)}), f32[65536,80]{0,1:T(8,128)}) %reduce-scatter.2.cloned.1.call-update) | async-done | bytes 20971536 | tf_op jit(solution)/shard_map/reduce_scatter | solution.py:40
  (28 shorter events, 0.2 us)
Async XLA Ops:
  8.0 3419.9 %all-reduce.3.cloned.1.call-start = ((), (), s32[]{:S(2)}) async-start(), calls=%async_computation.1 | async-start | bytes 1310720 | tf_op jit(solution)/shard_map/psum | solution.py:38
  9.2 59.3 %copy-start.4 = (f32[256]{0:T(256)}, f32[256]{0:T(256)S(1)}, u32[]{:S(2)}) copy-start(f32[256]{0:T(256)S(1)} %add_rsqrt_fusion) | copy-start | bytes 3076
  9.9 58.6 %copy-start.2 = (f32[640]{0:T(1024)}, f32[640]{0:T(1024)S(1)}, u32[]{:S(2)}) copy-start(f32[640]{0:T(1024)S(1)} %broadcast_add_fusion) | copy-start | bytes 7684
  1654.1 21.3 copy-start.1
  1654.2 21.3 copy-start.6
  1654.2 1010.7 %copy-start.8 = (f32[256]{0:T(256)S(1)}, f32[256]{0:T(256)}, u32[]{:S(2)}) copy-start(f32[256]{0:T(256)} %param.11) | copy-start | bytes 3076
  2722.6 44.4 %copy-start.7 = (s32[32,2,8,128]{3,1,2,0:T(2,128)S(1)}, s32[32,2,8,128]{3,1,2,0:T(2,128)}, u32[]{:S(2)}) copy-start(s32[32,2,8,128]{3,1,2,0:T(2,128)} %copy.12) | copy-start | bytes 786436
  3319.0 41.2 copy-start
  3319.0 41.2 copy-start.3
  3319.0 41.2 copy-start.5
  3360.1 978.0 %reduce-scatter.2.cloned.1.call-start = ((), (), s32[]{:S(2)}) async-start(), calls=%async_computation.2 | async-start | bytes 188743680 | tf_op jit(solution)/shard_map/reduce_scatter | solution.py:40
Sparse Core Ops, SparseCore 0:
  3360.2 53.9 all-reduce.2
Sparse Core Ops, SparseCore 1:
  3428.0 910.1 reduce-scatter.1
where the time goes:
time: 4400 us; the launch traced here: 4350 us
  local copies, waits for them, and re-layouts  1660 us (38%)
  blocking collectives  1030 us (23%)
  waiting for transfers between devices  893 us (20%)
  other arithmetic  587 us (13%)
  matrix products  164 us (4%)
    gather x3, local copies, waits for them, and re-layouts, local_head(): picked = jnp.take_along_axis(logits, safe_ids, axis=1)  1570 us
    psum x1, blocking collectives, local_head(): lax.psum(jnp.stack([jnp.sum(shifted, axis=1), teach_part], axis=1), 'tp')  989 us
    reduce_scatter x1, waiting for transfers between devices, local_head(): lax.psum_scatter(embed_part, 'dp', scatter_dimension=1, tiled=True)  893 us
    unnamed x8, other arithmetic  527 us
  transfers between devices with their start and end apart: 2, of which 1 were waited for; matrix products, arithmetic and copies ran while one was open for 2% of the time, Pallas kernels for 0%

commit v1 on v0

v1 whole, which is shorter than its diff:
```python
import functools

import jax
import jax.numpy as jnp
from jax import lax
from jax.experimental import pallas as pl
from jax.experimental.pallas import tpu as pltpu
from jax.sharding import PartitionSpec as P

EPS_NORM = 1e-6
LANES = 256
MIB = 1024 * 1024
NT = (((1,), (1,)), ((), ()))


def stats_kernel(emb_ref, ut_ref, max_ref, sum_ref, *, sub):
    @pl.when(pl.program_id(0) == 0)
    def _():
        max_ref[...] = jnp.full(max_ref.shape, -jnp.inf, jnp.float32)
        sum_ref[...] = jnp.zeros(sum_ref.shape, jnp.float32)

    rows = emb_ref.shape[0]
    toks = ut_ref.shape[1]
    for c in range(rows // sub):
        z = jnp.dot(emb_ref[c * sub:(c + 1) * sub, :], ut_ref[...], preferred_element_type=jnp.float32)
        z = z.reshape(sub // 8, 8, toks)
        old = max_ref[...]
        new = jnp.maximum(old, jnp.max(z, axis=0))
        sum_ref[...] = sum_ref[...] * jnp.exp(old - new) + jnp.sum(jnp.exp(z - new[None]), axis=0)
        max_ref[...] = new


def local_stats(emb, ut, rows=2048, sub=512):
    vocab, dim = emb.shape
    toks = ut.shape[1]
    shape = jax.ShapeDtypeStruct((8, toks), jnp.float32)
    return pl.pallas_call(
        functools.partial(stats_kernel, sub=sub),
        grid=(vocab // rows,),
        in_specs=[pl.BlockSpec((rows, dim), lambda i: (i, 0)), pl.BlockSpec((dim, toks), lambda i: (0, 0))],
        out_specs=[pl.BlockSpec((8, toks), lambda i: (0, 0))] * 2,
        out_shape=[shape, shape],
        compiler_params=pltpu.CompilerParams(vmem_limit_bytes=40 * MIB),
        cost_estimate=pl.CostEstimate(flops=2 * vocab * dim * toks, bytes_accessed=2 * vocab * dim, transcendentals=vocab * toks),
    )(emb, ut)


def teacher_kernel(base_ref, ids_ref, prob_ref, out_ref, *, high, group):
    top = ids_ref.shape[1]
    base = base_ref[0]
    high_iota = lax.broadcasted_iota(jnp.int32, (high, top), 0)
    low_iota = lax.broadcasted_iota(jnp.int32, (LANES, top), 0)

    def step(i, _):
        rows = pl.ds(pl.multiple_of(i * group, group), group)
        local = ids_ref[rows, :] - base
        hi = local >> 8
        lo = local & (LANES - 1)
        prob = prob_ref[rows, :]
        p1 = prob.astype(jnp.bfloat16).astype(jnp.float32)
        r1 = prob - p1
        p2 = r1.astype(jnp.bfloat16).astype(jnp.float32)
        p3 = r1 - p2
        parts = []
        for j in range(group):
            hit = high_iota == jnp.broadcast_to(hi[j:j + 1, :], (high, top))
            left = [jnp.where(hit, jnp.broadcast_to(p[j:j + 1, :], (high, top)), 0.0).astype(jnp.bfloat16) for p in (p1, p2, p3)]
            right = jnp.where(low_iota == jnp.broadcast_to(lo[j:j + 1, :], (LANES, top)), 1.0, 0.0).astype(jnp.bfloat16)
            dense = lax.dot_general(jnp.concatenate(left, axis=0), right, NT, preferred_element_type=jnp.float32)
            parts.append(dense[:high] + (dense[high:2 * high] + dense[2 * high:]))
        out_ref[:, rows, :] = jnp.swapaxes(jnp.stack(parts, axis=0), 0, 1)
        return 0

    lax.fori_loop(0, ids_ref.shape[0] // group, step, 0)


def teacher_dense(base, ids, prob, high, block=128):
    toks, top = ids.shape
    return pl.pallas_call(
        functools.partial(teacher_kernel, high=high, group=8),
        grid=(toks // block,),
        in_specs=[pl.BlockSpec(memory_space=pltpu.SMEM), pl.BlockSpec((block, top), lambda i: (i, 0)), pl.BlockSpec((block, top), lambda i: (i, 0))],
        out_specs=pl.BlockSpec((high, block, LANES), lambda i: (0, i, 0)),
        out_shape=jax.ShapeDtypeStruct((high, toks, LANES), jnp.float32),
        compiler_params=pltpu.CompilerParams(vmem_limit_bytes=40 * MIB),
        cost_estimate=pl.CostEstimate(flops=6 * high * LANES * toks * top, bytes_accessed=4 * high * LANES * toks, transcendentals=0),
    )(base, ids, prob)


def main_kernel(emb, dense, u_ref, ut_ref, logz_ref, w_ref, out, du_ref, tsum_ref,
                emb_buf, dense_buf, g_buf, de_buf, in_sem, send_sem, recv_sem, own_sem, *, tile, chunk, peers):
    toks, dim = u_ref.shape
    cols = dim // peers
    tp = lax.axis_index('tp')
    me = lax.axis_index('dp')
    block = emb.shape[0] // peers
    tiles = block // tile
    per = tile // LANES

    barrier = pltpu.get_barrier_semaphore()
    for s in range(1, peers):
        pl.semaphore_signal(barrier, inc=1, device_id=(tp, me ^ s), device_id_type=pl.DeviceIdType.MESH)
    pl.semaphore_wait(barrier, peers - 1)

    def fetch(t, slot):
        rows = pl.ds(pl.multiple_of(me * block + t * tile, tile), tile)
        return (
            pltpu.make_async_copy(emb.at[rows, :], emb_buf.at[slot], in_sem.at[slot, 0]),
            pltpu.make_async_copy(dense.at[pl.ds(t * per, per)], dense_buf.at[slot], in_sem.at[slot, 1]),
        )

    def send(t, s):
        to = me ^ s
        return pltpu.make_async_remote_copy(
            src_ref=de_buf.at[t, pl.ds(pl.multiple_of(to * cols, 8), cols), :],
            dst_ref=out.at[:, pl.ds(pl.multiple_of(me * block + t * tile, tile), tile)],
            send_sem=send_sem.at[t, s],
            recv_sem=recv_sem.at[t, s],
            device_id=(tp, to),
            device_id_type=pl.DeviceIdType.MESH,
        )

    def keep(t):
        return pltpu.make_async_copy(
            de_buf.at[t, pl.ds(pl.multiple_of(me * cols, 8), cols), :],
            out.at[:, pl.ds(pl.multiple_of(me * block + t * tile, tile), tile)],
            own_sem.at[t],
        )

    for c in fetch(0, 0):
        c.start()
    du_ref[...] = jnp.zeros(du_ref.shape, jnp.float32)
    tsum_ref[...] = jnp.zeros(tsum_ref.shape, jnp.float32)

    def step(t, _):
        slot = lax.rem(t, 2)
        for c in fetch(t, slot):
            c.wait()

        @pl.when(t + 1 < tiles)
        def _():
            for c in fetch(t + 1, 1 - slot):
                c.start()

        e = emb_buf[slot]

        def part(i, acc):
            rows = pl.ds(pl.multiple_of(i * chunk, chunk), chunk)
            z = lax.dot_general(u_ref[rows, :], e, NT, preferred_element_type=jnp.float32)
            w = w_ref[rows, :]
            logz = logz_ref[rows, :]
            for h in range(per):
                zh = z[:, h * LANES:(h + 1) * LANES]
                q = dense_buf[slot, h, rows, :] * w
                g_buf[rows, h * LANES:(h + 1) * LANES] = (jnp.exp(zh - logz) * w - q).astype(jnp.bfloat16)
                acc = acc + jnp.sum((q * zh).reshape(chunk // 8, 8, LANES), axis=0)
            du_ref[rows, :] += jnp.dot(g_buf[rows, :], e, preferred_element_type=jnp.float32)
            return acc

        tsum_ref[...] = lax.fori_loop(0, toks // chunk, part, tsum_ref[...])
        de_buf[t] = jnp.dot(ut_ref[...], g_buf[...], preferred_element_type=jnp.float32)
        keep(t).start()
        for s in range(1, peers):
            send(t, s).start()
        return 0

    lax.fori_loop(0, tiles, step, 0)

    def drain(t, _):
        keep(t).wait()
        for s in range(1, peers):
            send(t, s).wait()
        return 0

    lax.fori_loop(0, tiles, drain, 0)


def main_pass(emb, dense, u, ut, logz, w, peers, tile=512, chunk=512):
    vocab, dim = emb.shape
    toks = u.shape[0]
    block = vocab // peers
    tiles = block // tile
    per = tile // LANES
    vmem = pl.BlockSpec(memory_space=pltpu.VMEM)
    hbm = pl.BlockSpec(memory_space=pl.ANY)
    return pl.pallas_call(
        functools.partial(main_kernel, tile=tile, chunk=chunk, peers=peers),
        in_specs=[hbm, hbm, vmem, vmem, vmem, vmem],
        out_specs=[hbm, vmem, vmem],
        out_shape=[
            jax.ShapeDtypeStruct((dim // peers, vocab), jnp.float32),
            jax.ShapeDtypeStruct((toks, dim), jnp.float32),
            jax.ShapeDtypeStruct((8, LANES), jnp.float32),
        ],
        scratch_shapes=[
            pltpu.VMEM((2, tile, dim), jnp.bfloat16),
            pltpu.VMEM((2, per, toks, LANES), jnp.float32),
            pltpu.VMEM((toks, tile), jnp.bfloat16),
            pltpu.VMEM((tiles, dim, tile), jnp.float32),
            pltpu.SemaphoreType.DMA((2, 2)),
            pltpu.SemaphoreType.DMA((tiles, peers)),
            pltpu.SemaphoreType.DMA((tiles, peers)),
            pltpu.SemaphoreType.DMA((tiles,)),
        ],
        compiler_params=pltpu.CompilerParams(vmem_limit_bytes=63 * MIB, collective_id=0, has_side_effects=True),
        cost_estimate=pl.CostEstimate(flops=6 * block * dim * toks, bytes_accessed=4 * block * toks, transcendentals=block * toks),
    )(emb, dense, u, ut, logz, w)


def solution(mesh):
    peers = mesh.shape['dp']

    def local_head(hidden, embedding, norm_weight, teach_ids, teach_prob, tok_mask):
        vocab_local = embedding.shape[0]
        toks = hidden.shape[0]
        block = vocab_local // peers
        high = block // LANES
        dim = hidden.shape[1]
        tp = lax.axis_index('tp')
        dp = lax.axis_index('dp')
        scale_w = 1.0 + norm_weight
        h_f32 = hidden.astype(jnp.float32)
        inv_rms = lax.rsqrt(jnp.mean(h_f32 * h_f32, axis=1, keepdims=True) + EPS_NORM)
        normed = h_f32 * inv_rms

        ids_all = lax.all_gather(teach_ids, 'dp', axis=0, tiled=True)
        prob_all = lax.all_gather(teach_prob, 'dp', axis=0, tiled=True)
        normed_all = lax.all_gather(normed, 'dp', axis=0, tiled=True)

        u_loc = (normed * scale_w).astype(jnp.bfloat16)
        part_max, part_sum = local_stats(embedding, u_loc.T)
        loc_max = jnp.max(part_max, axis=0)
        loc_sum = jnp.sum(part_sum * jnp.exp(part_max - loc_max), axis=0)
        stats = lax.all_gather(jnp.stack([loc_max, loc_sum, tok_mask]), ('tp', 'dp'), axis=0, tiled=False)
        stats = stats.reshape(-1, peers, 3, toks)
        row_max = jnp.max(stats[:, :, 0], axis=0)
        sum_exp = jnp.sum(stats[:, :, 1] * jnp.exp(stats[:, :, 0] - row_max), axis=0)
        log_norm = (row_max + jnp.log(sum_exp)).reshape(-1, 1)
        mask = stats[0, :, 2].reshape(-1, 1)
        weight = mask / jnp.sum(mask)

        base = (tp * vocab_local + dp * block).astype(jnp.int32).reshape(1)
        dense = teacher_dense(base, ids_all, prob_all, high)
        u_all = (normed_all * scale_w).astype(jnp.bfloat16)
        de_t, du_part, tsum = main_pass(embedding, dense, u_all, u_all.T, log_norm, weight, peers)

        du_loc = lax.psum_scatter(du_part, 'dp', scatter_dimension=0, tiled=True)
        sums = jnp.concatenate([jnp.sum(du_loc * normed, axis=0), jnp.sum(tsum, axis=0)[:128], jnp.sum(tsum, axis=0)[128:]])
        sums = lax.psum(sums, ('tp', 'dp'))
        grad_norm = sums[:dim]
        loss_mean = jnp.sum(weight * log_norm) - jnp.sum(sums[dim:])
        grad_u = lax.psum(du_loc, 'tp')
        d_normed = grad_u * scale_w
        grad_hidden = (inv_rms * (d_normed - normed * jnp.mean(d_normed * normed, axis=1, keepdims=True))).astype(jnp.bfloat16)
        return loss_mean, grad_hidden, de_t.T, grad_norm

    return jax.shard_map(local_head, mesh=mesh, in_specs=(P('dp', None), P('tp', None), P(None), P('dp', None), P('dp', None), P('dp')), out_specs=(P(), P('dp', None), P('tp', 'dp'), P(None)), check_vma=False)
```

time: 4400 us -> 668 us (0.15); the launches traced: 4350 us -> 666 us
  local copies, waits for them, and re-layouts: 1660 us -> 32.1 us
  blocking collectives: 1030 us -> 83.4 us
  waiting for transfers between devices: 893 us -> 97.1 us
  other arithmetic: 587 us -> 14.4 us
  Pallas kernels: 0 us -> 423 us
  matrix products: 164 us -> 0 us
    gather x3 -> x0, local copies, waits for them, and re-layouts: 1570 us -> none  [local_head(): picked = jnp.take_along_axis(logits, safe_ids, axis=1)]
    psum x3 -> x1, blocking collectives: 1010 us -> 39.8 us  [local_head(): sums = lax.psum(sums, ('tp', 'dp'))]
    reduce_scatter x1, waiting for transfers between devices: 893 us -> 52.7 us  [local_head(): du_loc = lax.psum_scatter(du_part, 'dp', scatter_dimension=0, tiled=True)]
    unnamed x8 -> x3, other arithmetic: 527 us -> 1.35 us
    pallas_call x0 -> x3, Pallas kernels: none -> 423 us  [the longest x1 245 us: main_pass(): pl.pallas_call(functools.partial(main_kernel, tile=tile, chunk=chunk, pee...]
    dot_general x3 -> x0, matrix products: 164 us -> none  [the longest x1 67.7 us: local_head(): lax.dot_general(dlogit_bf, normed_bf, (((0,), (0,)), ((), ())), preferred...]
  transfers between devices with their start and end apart: 2 -> 5, of which waited for: 1 -> 2; matrix products, arithmetic and copies ran while one was open for 2% -> 1% of each run, Pallas kernels for 0% -> 27%
where the time goes in v1:
time: 668 us; the launch traced here: 666 us
  Pallas kernels  423 us (63%)
  waiting for transfers between devices  97.1 us (15%)
  blocking collectives  83.4 us (12%)
  local copies, waits for them, and re-layouts  32.1 us (5%)
  between operations  16.4 us (2%)
  other arithmetic  14.4 us (2%)
    pallas_call x1, Pallas kernels, main_pass(): pl.pallas_call(functools.partial(main_kernel, tile=tile, chunk=chunk, pee...  245 us
    pallas_call x1, Pallas kernels, teacher_dense(): pl.pallas_call(functools.partial(teacher_kernel, high=high, group=8), gri...  127 us
    reduce_scatter x1, waiting for transfers between devices, local_head(): du_loc = lax.psum_scatter(du_part, 'dp', scatter_dimension=0, tiled=True)  52.7 us
    pallas_call x1, Pallas kernels, local_stats(): pl.pallas_call(functools.partial(stats_kernel, sub=sub), grid=(vocab // r...  50.5 us
    all_gather x1, blocking collectives, local_head(): lax.all_gather(jnp.stack([loc_max, loc_sum, tok_mask]), ('tp', 'dp'), axi...  43.6 us
    psum x1, waiting for transfers between devices, local_head(): grad_u = lax.psum(du_loc, 'tp')  42.9 us
    psum x1, blocking collectives, local_head(): sums = lax.psum(sums, ('tp', 'dp'))  39.8 us
    unnamed x17, local copies, waits for them, and re-layouts  23.6 us
  transfers between devices with their start and end apart: 5, of which 2 were waited for; matrix products, arithmetic and copies ran while one was open for 1% of the time, Pallas kernels for 27%

profile of v1, /device:TPU:0, one launch (start us, length us, event | category | flops | bytes accessed | tf_op | source)
XLA Modules:
  0.0 666.1 jit_solution(4145305301594877802)
XLA Ops:
  7.2 0.7 all-gather.6.cloned.1.call-update
  7.9 0.0 all-gather.8.cloned.1.call-start
  7.9 0.7 all-gather.8.cloned.1.call-update
  8.6 0.0 all-gather.10.cloned.1.call-start
  8.7 1.1 copy.21
  9.8 0.1 fusion
  10.0 0.7 broadcast_add_fusion
  10.7 0.9 convert_multiply_fusion
  11.6 0.0 reduce-scatter.2.cloned.1.call-start
  11.7 50.5 %shard_map.93 = (f32[8,256]{1,0:T(8,128)S(1)}, f32[8,256]{1,0:T(8,128)S(1)}) custom-call(bf16[65536,640]{1,0:T(8,128)(2,1)} %emb.1, bf16[640,256]{1,0:T(8,128)(2,1)S(1)} %get-tuple-element.29.ut_ref), custom_call_target="tpu_custom_call" | custom-call | flops 21474836480 | bytes 83886080 | tf_op jit(solution)/shard_map/pallas_call | solution.py:37
  62.3 43.6 %all-gather.1 = f32[32,3,256]{2,1,0:T(4,128)S(1)} all-gather(f32[1,3,256]{2,1,0:T(4,128)S(1)} %maximum_bitcast_fusion), channel_id=2, replica_groups=mesh['tp'=4,'dp'=8] {'tp','dp'}, dimensions={0}, use_global_device_ids=true | all-gather | bytes 101376 | tf_op jit(solution)/shard_map/all_gather | solution.py:234
  106.0 0.6 slice_reduce_fusion.1
  106.6 1.3 fusion.7
  108.0 1.4 copy.29
  109.4 1.4 copy.31
  110.8 1.6 copy-done
  112.4 1.6 copy-done.1
  113.9 127.3 %shard_map.94.dense = f32[32,2048,256]{2,1,0:T(8,128)} custom-call(s32[1]{0:T(128)} %bitcast.9.base_ref, s32[2048,256]{1,0:T(8,128)S(1)} %copy-done, f32[2048,256]{1,0:T(8,128)S(1)} %copy-done.1), custom_call_target="tpu_custom_call" | custom-call | flops 25769803776 | bytes 67108864 | tf_op jit(solution)/shard_map/pallas_call | solution.py:79
  241.2 2.8 multiply_convert_fusion
  244.1 2.6 copy.23.u_ref
  246.6 4.3 fusion.8.ut_ref
  251.0 244.8 %shard_map.95 = (f32[80,65536]{1,0:T(8,128)}, f32[2048,640]{1,0:T(8,128)}, f32[8,256]{1,0:T(8,128)}) custom-call(bf16[65536,640]{1,0:T(8,128)(2,1)} %emb.1, f32[32,2048,256]{2,1,0:T(8,128)} %shard_map.94.dense, bf16[2048,640]{1,0:T(8,128)(2,1)} %copy.23.u_ref, bf16[640,2048]{1,0:T(8,128)(2,1)} %fusion.8.ut_ref, f32[2048,1]{1,0:T(8,128)} %bitcast.43, ...), custom_call_target="tpu_custom_call" | custom-call | flops 64424509440 | bytes 67108864 | tf_op jit(solution)/shard_map/pallas_call | solution.py:186
  495.8 5.9 copy.26
  501.7 0.0 all-reduce.2.cloned.1.call-start
  501.8 52.7 %reduce-scatter.2.cloned.1.call-done = f32[256,640]{0,1:T(8,128)} async-done(((f32[2048,640]{0,1:T(8,128)}), f32[256,640]{0,1:T(8,128)}) %reduce-scatter.2.cloned.1.call-update) | async-done | bytes 655376 | tf_op jit(solution)/shard_map/reduce_scatter | solution.py:247
  554.6 42.9 %all-reduce.2.cloned.1.call-done = f32[256,640]{0,1:T(8,128)} async-done(((f32[256,640]{0,1:T(8,128)}), f32[256,640]{0,1:T(8,128)}) %all-reduce.2.cloned.1.call-update) | async-done | bytes 655376 | tf_op jit(solution)/shard_map/psum | solution.py:252
  597.5 1.6 multiply_reduce_fusion
  599.1 1.2 multiply_convert_fusion.1
  600.3 0.9 copy.27
  601.2 39.8 %psum.14 = f32[896]{0:T(1024)S(1)} all-reduce(f32[896]{0:T(1024)S(1)} %pad_maximum_fusion), channel_id=1, replica_groups=mesh['tp'=4,'dp'=8] {'tp','dp'}, use_global_device_ids=true, to_apply=%region_10.0 | all-reduce | flops 896 | bytes 7168 | tf_op jit(solution)/shard_map/psum | solution.py:249
  641.0 0.6 slice_reduce_fusion.2
  642.9 15.6 %copy.36 = f32[65536,80]{0,1:T(8,128)} copy(f32[65536,80]{0,1:T(8,128)} %bitcast.42) | data formatting | bytes 41943040
  (28 shorter events, 0.3 us)
Async XLA Ops:
  7.2 103.6 %all-gather.6.cloned.1.call-start = ((), (), s32[]{:S(2)}) async-start(), calls=%async_computation.1 | async-start | bytes 2359296 | tf_op jit(solution)/shard_map/all_gather | solution.py:226
  7.9 102.9 %all-gather.8.cloned.1.call-start = ((), (), s32[]{:S(2)}) async-start(), calls=%async_computation.2 | async-start | bytes 2359296 | tf_op jit(solution)/shard_map/all_gather | solution.py:227
  8.6 232.6 %all-gather.10.cloned.1.call-start = ((), (), s32[]{:S(2)}) async-start(), calls=%async_computation.3 | async-start | bytes 5898240 | tf_op jit(solution)/shard_map/all_gather | solution.py:228
  11.6 542.9 %reduce-scatter.2.cloned.1.call-start = ((), (), s32[]{:S(2)}) async-start(), calls=%async_computation.4 | async-start | bytes 5898240 | tf_op jit(solution)/shard_map/reduce_scatter | solution.py:247
  11.7 50.6 %copy-start.4 = (f32[256]{0:T(256)S(1)}, f32[256]{0:T(256)}, u32[]{:S(2)}) copy-start(f32[256]{0:T(256)} %param.11) | copy-start | bytes 3076
  110.8 1.6 copy-start
  112.4 1.6 copy-start.1
  501.7 52.8 %copy-start.2 = (f32[8,256]{1,0:T(8,128)S(1)}, f32[8,256]{1,0:T(8,128)}, u32[]{:S(2)}) copy-start(f32[8,256]{1,0:T(8,128)} %get-tuple-element.12) | copy-start | bytes 24580
  501.7 95.8 %all-reduce.2.cloned.1.call-start = ((), (), s32[]{:S(2)}) async-start(), calls=%async_computation.5 | async-start | bytes 1310720 | tf_op jit(solution)/shard_map/psum | solution.py:252
  641.0 17.5 %copy-start.3 = (f32[896]{0:T(1024)}, f32[896]{0:T(1024)S(1)}, u32[]{:S(2)}) copy-start(f32[896]{0:T(1024)S(1)} %psum.14) | copy-start | bytes 10756
Sparse Core Ops, SparseCore 0:
  9.9 30.2 all-gather.5
  42.1 27.5 all-gather.7
  72.1 41.9 all-gather.9
  501.8 52.6 reduce-scatter.1
  556.7 40.7 all-reduce.1

commit v2 on v1

v2 whole, which is shorter than its diff:
```python
import functools

import jax
import jax.numpy as jnp
from jax import lax
from jax.experimental import pallas as pl
from jax.experimental.pallas import tpu as pltpu
from jax.sharding import PartitionSpec as P

EPS_NORM = 1e-6
LANES = 128
MIB = 1024 * 1024
NT = (((1,), (1,)), ((), ()))
MESH = pl.DeviceIdType.MESH


def swap_all(src, dst, send_sem, recv_sem, groups, peers):
    total = groups * peers
    me = lax.axis_index('tp') * peers + lax.axis_index('dp')

    def copy(s):
        to = lax.rem(me + s, total)
        return pltpu.make_async_remote_copy(
            src_ref=src, dst_ref=dst.at[me], send_sem=send_sem.at[s], recv_sem=recv_sem.at[s],
            device_id=(to // peers, lax.rem(to, peers)), device_id_type=MESH)

    def start(s, _):
        copy(s).start()
        return 0

    def wait(s, _):
        copy(s).wait()
        return 0

    return (lambda: lax.fori_loop(1, total, start, 0)), (lambda: lax.fori_loop(1, total, wait, 0))


def enter_all(groups, peers):
    total = groups * peers
    me = lax.axis_index('tp') * peers + lax.axis_index('dp')
    barrier = pltpu.get_barrier_semaphore()

    def greet(s, _):
        to = lax.rem(me + s, total)
        pl.semaphore_signal(barrier, inc=1, device_id=(to // peers, lax.rem(to, peers)), device_id_type=MESH)
        return 0

    lax.fori_loop(1, total, greet, 0)
    pl.semaphore_wait(barrier, total - 1)


def stats_kernel(emb_ref, ut_ref, mask_ref, out_ref, max_ref, sum_ref, mine_ref, all_ref, send_sem, recv_sem, *, sub, groups, peers):
    @pl.when(pl.program_id(0) == 0)
    def _():
        max_ref[...] = jnp.full(max_ref.shape, -jnp.inf, jnp.float32)
        sum_ref[...] = jnp.zeros(sum_ref.shape, jnp.float32)

    rows = emb_ref.shape[0]
    toks = ut_ref.shape[1]
    for c in range(rows // sub):
        z = jnp.dot(emb_ref[c * sub:(c + 1) * sub, :], ut_ref[...], preferred_element_type=jnp.float32)
        z = z.reshape(sub // 8, 8, toks)
        old = max_ref[...]
        new = jnp.maximum(old, jnp.max(z, axis=0))
        sum_ref[...] = sum_ref[...] * jnp.exp(old - new) + jnp.sum(jnp.exp(z - new[None]), axis=0)
        max_ref[...] = new

    @pl.when(pl.program_id(0) == pl.num_programs(0) - 1)
    def _():
        top = jnp.max(max_ref[...], axis=0, keepdims=True)
        tot = jnp.sum(sum_ref[...] * jnp.exp(max_ref[...] - top), axis=0, keepdims=True)
        row = lax.broadcasted_iota(jnp.int32, (8, toks), 0)
        mine = jnp.where(row == 0, top, jnp.where(row == 1, tot, mask_ref[...]))
        mine_ref[...] = mine
        me = lax.axis_index('tp') * peers + lax.axis_index('dp')
        all_ref[me] = mine
        enter_all(groups, peers)
        start, wait = swap_all(mine_ref, all_ref, send_sem, recv_sem, groups, peers)
        start()
        wait()
        out_ref[...] = all_ref[...]


def local_stats(emb, ut, mask, groups, peers, rows=2048, sub=512):
    vocab, dim = emb.shape
    toks = ut.shape[1]
    total = groups * peers
    return pl.pallas_call(
        functools.partial(stats_kernel, sub=sub, groups=groups, peers=peers),
        grid=(vocab // rows,),
        in_specs=[pl.BlockSpec((rows, dim), lambda i: (i, 0)), pl.BlockSpec((dim, toks), lambda i: (0, 0)), pl.BlockSpec((1, toks), lambda i: (0, 0))],
        out_specs=pl.BlockSpec((total, 8, toks), lambda i: (0, 0, 0)),
        out_shape=jax.ShapeDtypeStruct((total, 8, toks), jnp.float32),
        scratch_shapes=[pltpu.VMEM((8, toks), jnp.float32)] * 3 + [pltpu.VMEM((total, 8, toks), jnp.float32)] + [pltpu.SemaphoreType.DMA((total,))] * 2,
        compiler_params=pltpu.CompilerParams(vmem_limit_bytes=40 * MIB, collective_id=1, has_side_effects=True),
        cost_estimate=pl.CostEstimate(flops=2 * vocab * dim * toks, bytes_accessed=2 * vocab * dim, transcendentals=vocab * toks),
    )(emb, ut, mask)


def teacher_kernel(base_ref, ids_ref, prob_ref, out_ref, *, high, group):
    top = ids_ref.shape[1]
    base = base_ref[0]
    bf16 = jnp.bfloat16
    high_iota = lax.broadcasted_iota(jnp.int32, (high, top), 0).astype(jnp.float32).astype(bf16)
    low_iota = lax.broadcasted_iota(jnp.int32, (LANES, top), 0).astype(jnp.float32).astype(bf16)

    def spread(row, n):
        row = jnp.broadcast_to(row, (16, top)).astype(bf16)
        return jnp.broadcast_to(row[None], (n // 16, 16, top)).reshape(n, top)

    def step(i, _):
        rows = pl.ds(pl.multiple_of(i * group, group), group)
        local = ids_ref[rows, :] - base
        hi = local >> (LANES.bit_length() - 1)
        lo = (local & (LANES - 1)).astype(jnp.float32)
        hi = jnp.where((local >= 0) & (hi < high), hi, -1).astype(jnp.float32)
        prob = prob_ref[rows, :]
        p1 = prob.astype(bf16).astype(jnp.float32)
        r1 = prob - p1
        p2 = r1.astype(bf16).astype(jnp.float32)
        p3 = r1 - p2
        parts = []
        for j in range(group):
            hit = high_iota == spread(hi[j:j + 1, :], high)
            left = [jnp.where(hit, spread(p[j:j + 1, :], high), jnp.zeros((), bf16)) for p in (p1, p2, p3)]
            right = jnp.where(low_iota == spread(lo[j:j + 1, :], LANES), jnp.ones((), bf16), jnp.zeros((), bf16))
            dense = lax.dot_general(jnp.concatenate(left, axis=0), right, NT, preferred_element_type=jnp.float32)
            parts.append(dense[:high] + (dense[high:2 * high] + dense[2 * high:]))
        out_ref[:, rows, :] = jnp.swapaxes(jnp.stack(parts, axis=0), 0, 1)
        return 0

    lax.fori_loop(0, ids_ref.shape[0] // group, step, 0)


def teacher_dense(base, ids, prob, high, block=128):
    toks, top = ids.shape
    return pl.pallas_call(
        functools.partial(teacher_kernel, high=high, group=16),
        grid=(toks // block,),
        in_specs=[pl.BlockSpec(memory_space=pltpu.SMEM), pl.BlockSpec((block, top), lambda i: (i, 0)), pl.BlockSpec((block, top), lambda i: (i, 0))],
        out_specs=pl.BlockSpec((high, block, LANES), lambda i: (0, i, 0)),
        out_shape=jax.ShapeDtypeStruct((high, toks, LANES), jnp.float32),
        compiler_params=pltpu.CompilerParams(vmem_limit_bytes=40 * MIB),
        cost_estimate=pl.CostEstimate(flops=6 * high * LANES * toks * top, bytes_accessed=4 * high * LANES * toks, transcendentals=0),
    )(base, ids, prob)


def main_kernel(emb, dense, u_ref, ut_ref, logz_ref, w_ref, y_ref, out, du_full, sums_out,
                emb_buf, dense_buf, g_buf, de_buf, du_ref, tsum_ref, core_buf, z_buf, xy_buf, tot_ref, mine_ref, du_out, sums_ref,
                in_sem, send_sem, recv_sem, own_sem, red_send, red_recv, all_send, all_recv,
                *, tile, chunk, held, groups, peers):
    toks, dim = u_ref.shape
    cols = dim // peers
    local = toks // peers
    part_rows = local // groups
    tp = lax.axis_index('tp')
    me = lax.axis_index('dp')
    block = emb.shape[0] // peers
    tiles = block // tile
    per = tile // LANES
    pairs = peers // 2
    core = lax.rem(me, 2)
    chip = me // 2

    enter_all(groups, peers)

    def fetch(t, slot):
        rows = pl.ds(pl.multiple_of(me * block + t * tile, tile), tile)
        return (
            pltpu.make_async_copy(emb.at[rows, :], emb_buf.at[slot], in_sem.at[slot, 0]),
            pltpu.make_async_copy(dense.at[pl.ds(t * per, per)], dense_buf.at[slot], in_sem.at[slot, 1]),
        )

    def send(t, s):
        to = me ^ s
        return pltpu.make_async_remote_copy(
            src_ref=de_buf.at[t, pl.ds(pl.multiple_of(to * cols, 8), cols), :],
            dst_ref=out.at[:, pl.ds(pl.multiple_of(me * block + t * tile, tile), tile)],
            send_sem=send_sem.at[t, s],
            recv_sem=recv_sem.at[t, s],
            device_id=(tp, to),
            device_id_type=MESH,
        )

    def keep(t):
        return pltpu.make_async_copy(
            de_buf.at[t, pl.ds(pl.multiple_of(me * cols, 8), cols), :],
            out.at[:, pl.ds(pl.multiple_of(me * block + t * tile, tile), tile)],
            own_sem.at[t],
        )

    def send_tile(t):
        for s in range(peers - 1, 0, -1):
            send(t, s).start()

    for c in fetch(0, 0):
        c.start()
    du_ref[...] = jnp.zeros(du_ref.shape, jnp.float32)
    tsum_ref[...] = jnp.zeros(tsum_ref.shape, jnp.float32)

    def step(t, _):
        slot = lax.rem(t, 2)
        for c in fetch(t, slot):
            c.wait()

        @pl.when(t + 1 < tiles)
        def _():
            for c in fetch(t + 1, 1 - slot):
                c.start()

        e = emb_buf[slot]

        def part(i, acc):
            rows = pl.ds(pl.multiple_of(i * chunk, chunk), chunk)
            z = lax.dot_general(u_ref[rows, :], e, NT, preferred_element_type=jnp.float32)
            w = w_ref[rows, :]
            logz = logz_ref[rows, :]
            for h in range(per):
                zh = z[:, h * LANES:(h + 1) * LANES]
                q = dense_buf[slot, h, rows, :] * w
                g_buf[rows, h * LANES:(h + 1) * LANES] = (jnp.exp(zh - logz) * w - q).astype(jnp.bfloat16)
                acc = acc + jnp.sum((q * zh).reshape(chunk // 8, 8, LANES), axis=0)
            du_ref[rows, :] += jnp.dot(g_buf[rows, :], e, preferred_element_type=jnp.float32)
            return acc

        tsum_ref[...] = lax.fori_loop(0, toks // chunk, part, tsum_ref[...])
        de_buf[t] = jnp.dot(ut_ref[...], g_buf[...], preferred_element_type=jnp.float32)
        keep(t).start()

        @pl.when(t < tiles - held)
        def _():
            send_tile(t)

        return 0

    lax.fori_loop(0, tiles, step, 0)

    def to_core(q):
        rows = pl.ds(pl.multiple_of((2 * q + (1 - core)) * local, local), local)
        return pltpu.make_async_remote_copy(
            src_ref=du_ref.at[rows, :], dst_ref=core_buf.at[q], send_sem=red_send.at[q], recv_sem=red_recv.at[q],
            device_id=(tp, me ^ 1), device_id_type=MESH)

    for q in range(pairs):
        to_core(q).start()
    for q in range(pairs):
        to_core(q).wait()
    for q in range(pairs):
        core_buf[q] += du_ref[pl.ds(pl.multiple_of((2 * q + core) * local, local), local), :]

    def to_z(s):
        there = tp ^ s
        return pltpu.make_async_remote_copy(
            src_ref=core_buf.at[:, pl.ds(pl.multiple_of(there * part_rows, part_rows), part_rows), :], dst_ref=z_buf.at[s],
            send_sem=red_send.at[pairs + s], recv_sem=red_recv.at[pairs + s],
            device_id=(there, me), device_id_type=MESH)

    for s in range(1, groups):
        to_z(s).start()
    for s in range(1, groups):
        to_z(s).wait()
    mine = core_buf[:, pl.ds(pl.multiple_of(tp * part_rows, part_rows), part_rows), :]
    for s in range(1, groups):
        mine += z_buf[s]
    z_buf[0] = mine

    def to_chip(s):
        there = chip ^ s
        return pltpu.make_async_remote_copy(
            src_ref=z_buf.at[0, there], dst_ref=xy_buf.at[s],
            send_sem=red_send.at[pairs + groups + s], recv_sem=red_recv.at[pairs + groups + s],
            device_id=(tp, 2 * there + core), device_id_type=MESH)

    for s in range(1, pairs):
        to_chip(s).start()

    def late(t, _):
        send_tile(t)
        return 0

    lax.fori_loop(tiles - held, tiles, late, 0)
    for s in range(1, pairs):
        to_chip(s).wait()
    total = z_buf[0, chip]
    for s in range(1, pairs):
        total += xy_buf[s]
    tot_ref[...] = total
    here = pl.ds(pl.multiple_of(tp * part_rows, part_rows), part_rows)
    du_out[here, :] = total

    def share(s):
        return pltpu.make_async_remote_copy(
            src_ref=tot_ref, dst_ref=du_out.at[here, :],
            send_sem=red_send.at[2 * pairs + groups + s], recv_sem=red_recv.at[2 * pairs + groups + s],
            device_id=(tp ^ s, me), device_id_type=MESH)

    for s in range(1, groups):
        share(s).start()

    dw = jnp.sum(total * y_ref[here, :], axis=0, keepdims=True)
    rows = [dw[:, i * 128:(i + 1) * 128] for i in range(dim // 128)]
    rows.append(jnp.sum(tsum_ref[...], axis=0, keepdims=True))
    rows.append(jnp.zeros((16 - len(rows), 128), jnp.float32))
    sums = jnp.concatenate(rows, axis=0)
    mine_ref[...] = sums
    sums_ref[tp * peers + me] = sums
    start, wait = swap_all(mine_ref, sums_ref, all_send, all_recv, groups, peers)
    start()
    for s in range(1, groups):
        share(s).wait()
    du_full[...] = du_out[...]
    wait()
    sums_out[...] = jnp.sum(sums_ref[...], axis=0)

    def drain(t, _):
        keep(t).wait()
        for s in range(1, peers):
            send(t, s).wait()
        return 0

    lax.fori_loop(0, tiles, drain, 0)


def main_pass(emb, dense, u, ut, logz, w, y, groups, peers, tile=512, chunk=512, held=3):
    vocab, dim = emb.shape
    toks = u.shape[0]
    block = vocab // peers
    tiles = block // tile
    per = tile // LANES
    total = groups * peers
    local = toks // peers
    pairs = peers // 2
    f32 = jnp.float32
    vmem = pl.BlockSpec(memory_space=pltpu.VMEM)
    hbm = pl.BlockSpec(memory_space=pl.ANY)
    red = 2 * pairs + 2 * groups
    return pl.pallas_call(
        functools.partial(main_kernel, tile=tile, chunk=chunk, held=held, groups=groups, peers=peers),
        in_specs=[hbm, hbm, vmem, vmem, vmem, vmem, vmem],
        out_specs=[hbm, vmem, vmem],
        out_shape=[
            jax.ShapeDtypeStruct((dim // peers, vocab), f32),
            jax.ShapeDtypeStruct((local, dim), f32),
            jax.ShapeDtypeStruct((16, 128), f32),
        ],
        scratch_shapes=[
            pltpu.VMEM((2, tile, dim), jnp.bfloat16),
            pltpu.VMEM((2, per, toks, LANES), f32),
            pltpu.VMEM((toks, tile), jnp.bfloat16),
            pltpu.VMEM((tiles, dim, tile), f32),
            pltpu.VMEM((toks, dim), f32),
            pltpu.VMEM((8, LANES), f32),
            pltpu.VMEM((pairs, local, dim), f32),
            pltpu.VMEM((groups, pairs, local // groups, dim), f32),
            pltpu.VMEM((pairs, local // groups, dim), f32),
            pltpu.VMEM((local // groups, dim), f32),
            pltpu.VMEM((16, 128), f32),
            pltpu.VMEM((local, dim), f32),
            pltpu.VMEM((total, 16, 128), f32),
            pltpu.SemaphoreType.DMA((2, 2)),
            pltpu.SemaphoreType.DMA((tiles, peers)),
            pltpu.SemaphoreType.DMA((tiles, peers)),
            pltpu.SemaphoreType.DMA((tiles,)),
            pltpu.SemaphoreType.DMA((red,)),
            pltpu.SemaphoreType.DMA((red,)),
            pltpu.SemaphoreType.DMA((total,)),
            pltpu.SemaphoreType.DMA((total,)),
        ],
        compiler_params=pltpu.CompilerParams(vmem_limit_bytes=63 * MIB, collective_id=0, has_side_effects=True),
        cost_estimate=pl.CostEstimate(flops=6 * block * dim * toks, bytes_accessed=4 * block * toks, transcendentals=block * toks),
    )(emb, dense, u, ut, logz, w, y)


def solution(mesh):
    peers = mesh.shape['dp']
    groups = mesh.shape['tp']

    def local_head(hidden, embedding, norm_weight, teach_ids, teach_prob, tok_mask):
        vocab_local = embedding.shape[0]
        toks = hidden.shape[0]
        block = vocab_local // peers
        high = block // LANES
        dim = hidden.shape[1]
        tp = lax.axis_index('tp')
        dp = lax.axis_index('dp')
        scale_w = 1.0 + norm_weight
        h_f32 = hidden.astype(jnp.float32)
        inv_rms = lax.rsqrt(jnp.mean(h_f32 * h_f32, axis=1, keepdims=True) + EPS_NORM)
        normed = h_f32 * inv_rms

        ids_all = lax.all_gather(teach_ids, 'dp', axis=0, tiled=True)
        prob_all = lax.all_gather(teach_prob, 'dp', axis=0, tiled=True)
        normed_all = lax.all_gather(normed, 'dp', axis=0, tiled=True)

        u_loc = (normed * scale_w).astype(jnp.bfloat16)
        stats = local_stats(embedding, u_loc.T, tok_mask.reshape(1, -1), groups, peers)
        stats = stats.reshape(groups, peers, 8, toks)
        row_max = jnp.max(stats[:, :, 0], axis=0)
        sum_exp = jnp.sum(stats[:, :, 1] * jnp.exp(stats[:, :, 0] - row_max), axis=0)
        log_norm = (row_max + jnp.log(sum_exp)).reshape(-1, 1)
        mask = stats[0, :, 2].reshape(-1, 1)
        weight = mask / jnp.sum(mask)

        base = (tp * vocab_local + dp * block).astype(jnp.int32).reshape(1)
        dense = teacher_dense(base, ids_all, prob_all, high)
        u_all = (normed_all * scale_w).astype(jnp.bfloat16)
        de_t, grad_u, sums = main_pass(embedding, dense, u_all, u_all.T, log_norm, weight, normed, groups, peers)
        used = dim // 128
        grad_norm = sums[:used].reshape(dim)
        loss_mean = jnp.sum(weight * log_norm) - jnp.sum(sums[used])
        d_normed = grad_u * scale_w
        grad_hidden = (inv_rms * (d_normed - normed * jnp.mean(d_normed * normed, axis=1, keepdims=True))).astype(jnp.bfloat16)
        return loss_mean, grad_hidden, de_t.T, grad_norm

    return jax.shard_map(local_head, mesh=mesh, in_specs=(P('dp', None), P('tp', None), P(None), P('dp', None), P('dp', None), P('dp')), out_specs=(P(), P('dp', None), P('tp', 'dp'), P(None)), check_vma=False)
```

time: 668 us -> 470 us (0.70)
  waiting for transfers between devices: 97.1 us -> 1.4 us
  blocking collectives: 83.4 us -> 0 us
  Pallas kernels: 423 us -> 406 us
    reduce_scatter x1 -> x0, waiting for transfers between devices: 52.7 us -> none  [local_head(): du_loc = lax.psum_scatter(du_part, 'dp', scatter_dimension=0, tiled=True)]
    all_gather x1 -> x0, blocking collectives: 43.6 us -> none  [local_head(): lax.all_gather(jnp.stack([loc_max, loc_sum, tok_mask]), ('tp', 'dp'), axi...]
    psum x1 -> x0, waiting for transfers between devices: 42.9 us -> none  [local_head(): grad_u = lax.psum(du_loc, 'tp')]
    psum x1 -> x0, blocking collectives: 39.8 us -> none  [local_head(): sums = lax.psum(sums, ('tp', 'dp'))]
    pallas_call x3, Pallas kernels: 423 us -> 406 us  [the longest x1 260 us: main_pass(): pl.pallas_call(functools.partial(main_kernel, tile=tile, chunk=chunk, hel...]
    unnamed x17 -> x13, local copies, waits for them, and re-layouts: 23.6 us -> 22.2 us
  transfers between devices with their start and end apart: 5 -> 3, of which waited for: 2 -> 0; matrix products, arithmetic and copies ran while one was open for 1% -> 2% of each run, Pallas kernels for 27% -> 31%
where the time goes in v2:
time: 470 us; the launch traced here: 468 us
  Pallas kernels  406 us (86%)
  local copies, waits for them, and re-layouts  26.4 us (6%)
  other arithmetic  17.7 us (4%)
  between operations  16.2 us (3%)
    pallas_call x1, Pallas kernels, main_pass(): pl.pallas_call(functools.partial(main_kernel, tile=tile, chunk=chunk, hel...  260 us
    pallas_call x1, Pallas kernels, teacher_dense(): pl.pallas_call(functools.partial(teacher_kernel, high=high, group=16), gr...  82.6 us
    pallas_call x1, Pallas kernels, local_stats(): pl.pallas_call(functools.partial(stats_kernel, sub=sub, groups=groups, pe...  63.3 us
    unnamed x13, local copies, waits for them, and re-layouts  22.2 us
  transfers between devices with their start and end apart: 3, of which 0 were waited for; matrix products, arithmetic and copies ran while one was open for 2% of the time, Pallas kernels for 31%

profile of v2, /device:TPU:0, one launch (start us, length us, event | category | flops | bytes accessed | tf_op | source)
XLA Modules:
  0.0 468.2 jit_solution(11142958532282301695)
XLA Ops:
  7.2 0.0 all-gather.4.cloned.1.call-start
  7.2 0.7 all-gather.4.cloned.1.call-update
  7.9 0.0 all-gather.6.cloned.1.call-start
  7.9 0.7 all-gather.6.cloned.1.call-update
  8.6 0.0 all-gather.8.cloned.1.call-start
  8.7 1.1 fusion
  9.8 0.7 broadcast_add_fusion
  10.5 2.0 convert_multiply_fusion
  12.5 0.0 all-gather.8.cloned.1.call-update
  12.5 0.2 copy.14.ut_ref
  12.7 0.0 copy-start
  12.7 0.7 copy-done
  13.4 63.3 %shard_map.93 = f32[32,8,256]{2,1,0:T(8,128)S(1)} custom-call(bf16[65536,640]{1,0:T(8,128)(2,1)} %emb.1, bf16[640,256]{1,0:T(8,128)(2,1)S(1)} %copy.14.ut_ref, f32[1,256]{1,0:T(1,128)S(1)} %bitcast.39), custom_call_target="tpu_custom_call" | custom-call | flops 21474836480 | bytes 83886080 | tf_op jit(solution)/shard_map/pallas_call | solution.py:88
  76.7 0.1 fusion.10
  76.8 0.6 fusion.9
  77.4 1.3 fusion.8
  78.7 1.4 copy.26
  80.1 1.4 copy.28
  81.5 0.0 all-gather.4.cloned.1.call-done.ids_ref
  81.5 1.6 copy-done.1
  83.1 1.6 copy-done.2
  84.7 82.6 %shard_map.94.dense = f32[64,2048,128]{2,1,0:T(8,128)} custom-call(s32[1]{0:T(128)} %bitcast.5.base_ref, s32[2048,256]{1,0:T(8,128)S(1)} %copy-done.1, f32[2048,256]{1,0:T(8,128)S(1)} %copy-done.2), custom_call_target="tpu_custom_call" | custom-call | flops 25769803776 | bytes 67108864 | tf_op jit(solution)/shard_map/pallas_call | solution.py:137
  167.4 2.9 fusion.11
  170.2 2.7 copy.17.ut_ref
  173.0 4.4 multiply_convert_fusion.u_ref
  177.4 260.5 %shard_map.95 = (f32[80,65536]{1,0:T(8,128)}, f32[256,640]{1,0:T(8,128)}, f32[16,128]{1,0:T(8,128)}) custom-call(bf16[65536,640]{1,0:T(8,128)(2,1)} %emb.1, f32[64,2048,128]{2,1,0:T(8,128)} %shard_map.94.dense, bf16[2048,640]{1,0:T(8,128)(2,1)} %multiply_convert_fusion.u_ref, bf16[640,2048]{1,0:T(8,128)(2,1)} %copy.17.ut_ref, f32[2048,1]{1,0:T(8,128)} %bitcast.41, ...), custom_call_target="tpu_custom_call" | custom-call | flops 64424509440 | bytes 67108864 | tf_op jit(solution)/shard_map/pallas_call | solution.py:337
  437.9 1.3 slice_reduce_fusion
  439.2 1.3 slice_bitcast_fusion
  440.4 0.0 copy-done.3
  440.4 1.3 multiply_reduce_fusion
  441.8 2.0 multiply_convert_fusion.1
  445.0 15.6 %copy.45 = f32[65536,80]{0,1:T(8,128)} copy(f32[65536,80]{0,1:T(8,128)} %bitcast.40) | data formatting | bytes 41943040
  (11 shorter events, 0.1 us)
Async XLA Ops:
  7.2 74.4 %all-gather.4.cloned.1.call-start = ((), (), s32[]{:S(2)}) async-start(), calls=%async_computation | async-start | bytes 2359296 | tf_op jit(solution)/shard_map/all_gather | solution.py:391
  7.9 73.6 %all-gather.6.cloned.1.call-start = ((), (), s32[]{:S(2)}) async-start(), calls=%async_computation.1 | async-start | bytes 2359296 | tf_op jit(solution)/shard_map/all_gather | solution.py:392
  8.6 158.7 %all-gather.8.cloned.1.call-start = ((), (), s32[]{:S(2)}) async-start(), calls=%async_computation.2 | async-start | bytes 5898240 | tf_op jit(solution)/shard_map/all_gather | solution.py:393
  12.7 0.7 copy-start
  81.5 1.6 copy-start.1
  83.1 1.6 copy-start.2
  177.4 263.1 %copy-start.3 = (bf16[256,640]{1,0:T(8,128)(2,1)S(1)}, bf16[256,640]{1,0:T(8,128)(2,1)}, u32[]{:S(2)}) copy-start(bf16[256,640]{1,0:T(8,128)(2,1)} %param.6) | copy-start | bytes 983044
Sparse Core Ops, SparseCore 0:
  9.9 30.2 all-gather.3
  42.0 27.5 all-gather.5
  71.5 40.8 all-gather.7

commit v3 on v2

--- a/solution.py
+++ b/solution.py
@@ -9,6 +9,8 @@
 
 EPS_NORM = 1e-6
 LANES = 128
+TILE = 512
+OWN = 8
 MIB = 1024 * 1024
 NT = (((1,), (1,)), ((), ()))
 MESH = pl.DeviceIdType.MESH
@@ -81,7 +83,7 @@
         out_ref[...] = all_ref[...]
 
 
-def local_stats(emb, ut, mask, groups, peers, rows=2048, sub=512):
+def local_stats(emb, ut, mask, groups, peers, rows=8192, sub=1024):
     vocab, dim = emb.shape
     toks = ut.shape[1]
     total = groups * peers
@@ -97,9 +99,9 @@
     )(emb, ut, mask)
 
 
-def teacher_kernel(base_ref, ids_ref, prob_ref, out_ref, *, high, group):
+def teacher_kernel(base_ref, ids_ref, prob_ref, out_ref, *, regions, group):
     top = ids_ref.shape[1]
-    base = base_ref[0]
+    high = sum(regions)
     bf16 = jnp.bfloat16
     high_iota = lax.broadcasted_iota(jnp.int32, (high, top), 0).astype(jnp.float32).astype(bf16)
     low_iota = lax.broadcasted_iota(jnp.int32, (LANES, top), 0).astype(jnp.float32).astype(bf16)
@@ -110,10 +112,15 @@
 
     def step(i, _):
         rows = pl.ds(pl.multiple_of(i * group, group), group)
-        local = ids_ref[rows, :] - base
-        hi = local >> (LANES.bit_length() - 1)
-        lo = (local & (LANES - 1)).astype(jnp.float32)
-        hi = jnp.where((local >= 0) & (hi < high), hi, -1).astype(jnp.float32)
+        ids = ids_ref[rows, :]
+        lo = (ids & (LANES - 1)).astype(jnp.float32)
+        hi = jnp.full(ids.shape, -1, jnp.int32)
+        first = 0
+        for r, size in enumerate(regions):
+            local = (ids >> (LANES.bit_length() - 1)) - base_ref[r]
+            hi = jnp.where((local >= 0) & (local < size), local + first, hi)
+            first += size
+        hi = hi.astype(jnp.float32)
         prob = prob_ref[rows, :]
         p1 = prob.astype(bf16).astype(jnp.float32)
         r1 = prob - p1
@@ -132,10 +139,11 @@
     lax.fori_loop(0, ids_ref.shape[0] // group, step, 0)
 
 
-def teacher_dense(base, ids, prob, high, block=128):
+def teacher_dense(base, ids, prob, regions, block=128):
+    high = sum(regions)
     toks, top = ids.shape
     return pl.pallas_call(
-        functools.partial(teacher_kernel, high=high, group=16),
+        functools.partial(teacher_kernel, regions=regions, group=64),
         grid=(toks // block,),
         in_specs=[pl.BlockSpec(memory_space=pltpu.SMEM), pl.BlockSpec((block, top), lambda i: (i, 0)), pl.BlockSpec((block, top), lambda i: (i, 0))],
         out_specs=pl.BlockSpec((high, block, LANES), lambda i: (0, i, 0)),
@@ -146,94 +154,152 @@
 
 
 def main_kernel(emb, dense, u_ref, ut_ref, logz_ref, w_ref, y_ref, out, du_full, sums_out,
-                emb_buf, dense_buf, g_buf, de_buf, du_ref, tsum_ref, core_buf, z_buf, xy_buf, tot_ref, mine_ref, du_out, sums_ref,
-                in_sem, send_sem, recv_sem, own_sem, red_send, red_recv, all_send, all_recv,
-                *, tile, chunk, held, groups, peers):
+                emb_buf, dense_buf, g_buf, ut_half, de_buf, de_half, du_ref, tsum_ref, core_buf, z_buf, xy_buf, tot_ref, mine_ref, du_out, sums_ref,
+                in_sem, send_sem, recv_sem, own_sem, half_send, half_recv, half_own, red_send, red_recv, all_send, all_recv,
+                *, tile, own, shared, held, groups, peers):
     toks, dim = u_ref.shape
     cols = dim // peers
     local = toks // peers
     part_rows = local // groups
     tp = lax.axis_index('tp')
     me = lax.axis_index('dp')
-    block = emb.shape[0] // peers
-    tiles = block // tile
     per = tile // LANES
     pairs = peers // 2
     core = lax.rem(me, 2)
     chip = me // 2
+    x_pos = lax.rem(chip, 2)
+    y_pos = chip // 2
+    chunk = toks // 2
+    wide = dim // 2
 
     enter_all(groups, peers)
 
-    def fetch(t, slot):
-        rows = pl.ds(pl.multiple_of(me * block + t * tile, tile), tile)
+    def first_row(k, i):
+        index = (me * own, peers * own + (2 * y_pos + core) * shared, peers * own + pairs * shared + (2 * x_pos + core) * shared)[k]
+        return pl.multiple_of((index + i) * tile, tile)
+
+    def fetch(k, i, slot):
+        plane = ((0, own, own + shared)[k] + i) * per
         return (
-            pltpu.make_async_copy(emb.at[rows, :], emb_buf.at[slot], in_sem.at[slot, 0]),
-            pltpu.make_async_copy(dense.at[pl.ds(t * per, per)], dense_buf.at[slot], in_sem.at[slot, 1]),
+            pltpu.make_async_copy(emb.at[pl.ds(first_row(k, i), tile), :], emb_buf.at[slot], in_sem.at[slot, 0]),
+            pltpu.make_async_copy(dense.at[pl.ds(plane, per)], dense_buf.at[slot], in_sem.at[slot, 1]),
         )
 
-    def send(t, s):
+    def begin(k, i, slot):
+        for c in fetch(k, i, slot):
+            c.start()
+
+    def arrive(k, i, slot):
+        for c in fetch(k, i, slot):
+            c.wait()
+
+    def send(i, s):
         to = me ^ s
         return pltpu.make_async_remote_copy(
-            src_ref=de_buf.at[t, pl.ds(pl.multiple_of(to * cols, 8), cols), :],
-            dst_ref=out.at[:, pl.ds(pl.multiple_of(me * block + t * tile, tile), tile)],
-            send_sem=send_sem.at[t, s],
-            recv_sem=recv_sem.at[t, s],
-            device_id=(tp, to),
-            device_id_type=MESH,
-        )
-
-    def keep(t):
+            src_ref=de_buf.at[i, pl.ds(pl.multiple_of(to * cols, 8), cols), :],
+            dst_ref=out.at[:, pl.ds(first_row(0, i), tile)],
+            send_sem=send_sem.at[i, s], recv_sem=recv_sem.at[i, s],
+            device_id=(tp, to), device_id_type=MESH)
+
+    def keep(i):
         return pltpu.make_async_copy(
-            de_buf.at[t, pl.ds(pl.multiple_of(me * cols, 8), cols), :],
-            out.at[:, pl.ds(pl.multiple_of(me * block + t * tile, tile), tile)],
-            own_sem.at[t],
-        )
-
-    def send_tile(t):
-        for s in range(peers - 1, 0, -1):
-            send(t, s).start()
-
-    for c in fetch(0, 0):
-        c.start()
+            de_buf.at[i, pl.ds(pl.multiple_of(me * cols, 8), cols), :],
+            out.at[:, pl.ds(first_row(0, i), tile)], own_sem.at[i])
+
+    def place(k, dev):
+        far = dev // pairs if k == 1 else lax.rem(dev // 2, 2)
+        return pl.multiple_of((2 * far + lax.rem(dev, 2)) * cols, 8)
+
+    def send_half(k, i, s):
+        to = me ^ ((s & 1) + (s >> 1) * (pairs if k == 1 else 2))
+        return pltpu.make_async_remote_copy(
+            src_ref=de_half.at[k - 1, i, pl.ds(place(k, to), cols), :],
+            dst_ref=out.at[:, pl.ds(first_row(k, i), tile)],
+            send_sem=half_send.at[k - 1, i, s], recv_sem=half_recv.at[k - 1, i, s],
+            device_id=(tp, to), device_id_type=MESH)
+
+    def keep_half(k, i):
+        return pltpu.make_async_copy(
+            de_half.at[k - 1, i, pl.ds(place(k, me), cols), :],
+            out.at[:, pl.ds(first_row(k, i), tile)], half_own.at[k - 1, i])
+
+    begin(0, 0, 0)
     du_ref[...] = jnp.zeros(du_ref.shape, jnp.float32)
     tsum_ref[...] = jnp.zeros(tsum_ref.shape, jnp.float32)
-
-    def step(t, _):
-        slot = lax.rem(t, 2)
-        for c in fetch(t, slot):
-            c.wait()
-
-        @pl.when(t + 1 < tiles)
+    quarter = dim // 4
+    for j in range(2):
+        lines = pl.ds(pl.multiple_of(j * wide + x_pos * quarter, 16), quarter)
+        ut_half[0, j * quarter:(j + 1) * quarter, :] = ut_ref[lines, :]
+    ut_half[1] = ut_ref[pl.ds(pl.multiple_of(y_pos * wide, 16), wide), :]
+
+    def gradient(rows, slot, counted):
+        e = emb_buf[slot]
+        z = lax.dot_general(u_ref[rows, :], e, NT, preferred_element_type=jnp.float32)
+        w = w_ref[rows, :]
+        logz = logz_ref[rows, :]
+        acc = jnp.zeros((8, LANES), jnp.float32)
+        for h in range(per):
+            zh = z[:, h * LANES:(h + 1) * LANES]
+            q = dense_buf[slot, h, rows, :] * w
+            g_buf[rows, h * LANES:(h + 1) * LANES] = (jnp.exp(zh - logz) * w - q).astype(jnp.bfloat16)
+            if counted:
+                acc = acc + jnp.sum((q * zh).reshape(chunk // 8, 8, LANES), axis=0)
+        if counted:
+            tsum_ref[...] += acc
+            du_ref[rows, :] += jnp.dot(g_buf[rows, :], e, preferred_element_type=jnp.float32)
+
+    def own_step(i, _):
+        slot = lax.rem(i, 2)
+        arrive(0, i, slot)
+
+        @pl.when(i + 1 < own)
         def _():
-            for c in fetch(t + 1, 1 - slot):
-                c.start()
-
-        e = emb_buf[slot]
-
-        def part(i, acc):
-            rows = pl.ds(pl.multiple_of(i * chunk, chunk), chunk)
-            z = lax.dot_general(u_ref[rows, :], e, NT, preferred_element_type=jnp.float32)
-            w = w_ref[rows, :]
-            logz = logz_ref[rows, :]
-            for h in range(per):
-                zh = z[:, h * LANES:(h + 1) * LANES]
-                q = dense_buf[slot, h, rows, :] * w
-                g_buf[rows, h * LANES:(h + 1) * LANES] = (jnp.exp(zh - logz) * w - q).astype(jnp.bfloat16)
-                acc = acc + jnp.sum((q * zh).reshape(chunk // 8, 8, LANES), axis=0)
-            du_ref[rows, :] += jnp.dot(g_buf[rows, :], e, preferred_element_type=jnp.float32)
-            return acc
-
-        tsum_ref[...] = lax.fori_loop(0, toks // chunk, part, tsum_ref[...])
-        de_buf[t] = jnp.dot(ut_ref[...], g_buf[...], preferred_element_type=jnp.float32)
-        keep(t).start()
-
-        @pl.when(t < tiles - held)
+            begin(0, i + 1, 1 - slot)
+
+        @pl.when(i + 1 == own)
         def _():
-            send_tile(t)
-
-        return 0
-
-    lax.fori_loop(0, tiles, step, 0)
+            begin(1, 0, 0)
+
+        def part(c, _):
+            gradient(pl.ds(pl.multiple_of(c * chunk, chunk), chunk), slot, True)
+            return 0
+
+        lax.fori_loop(0, 2, part, 0)
+        de_buf[i] = jnp.dot(ut_ref[...], g_buf[...], preferred_element_type=jnp.float32)
+        keep(i).start()
+        for s in range(peers - 1, 0, -1):
+            send(i, s).start()
+        return 0
+
+    lax.fori_loop(0, own, own_step, 0)
+
+    def send_shared(i):
+        for k in (1, 2):
+            for s in (3, 2, 1):
+                send_half(k, i, s).start()
+
+    def shared_step(i, _):
+        for k, half in ((1, x_pos), (2, y_pos)):
+            slot = k - 1
+            arrive(k, i, slot)
+            if k == 1:
+                begin(2, i, 1)
+            else:
+                @pl.when(i + 1 < shared)
+                def _():
+                    begin(1, i + 1, 0)
+            gradient(pl.ds(pl.multiple_of((1 - half) * chunk, chunk), chunk), slot, False)
+            gradient(pl.ds(pl.multiple_of(half * chunk, chunk), chunk), slot, True)
+            de_half[k - 1, i] = jnp.dot(ut_half[k - 1], g_buf[...], preferred_element_type=jnp.float32)
+            keep_half(k, i).start()
+
+        @pl.when(i < shared - held)
+        def _():
+            send_shared(i)
+
+        return 0
+
+    lax.fori_loop(0, shared, shared_step, 0)
 
     def to_core(q):
         rows = pl.ds(pl.multiple_of((2 * q + (1 - core)) * local, local), local)
@@ -274,11 +340,11 @@
     for s in range(1, pairs):
         to_chip(s).start()
 
-    def late(t, _):
-        send_tile(t)
-        return 0
-
-    lax.fori_loop(tiles - held, tiles, late, 0)
+    def late(i, _):
+        send_shared(i)
+        return 0
+
+    lax.fori_loop(shared - held, shared, late, 0)
     for s in range(1, pairs):
         to_chip(s).wait()
     total = z_buf[0, chip]
@@ -312,20 +378,27 @@
     wait()
     sums_out[...] = jnp.sum(sums_ref[...], axis=0)
 
-    def drain(t, _):
-        keep(t).wait()
+    def drain(i, _):
+        keep(i).wait()
         for s in range(1, peers):
-            send(t, s).wait()
-        return 0
-
-    lax.fori_loop(0, tiles, drain, 0)
-
-
-def main_pass(emb, dense, u, ut, logz, w, y, groups, peers, tile=512, chunk=512, held=3):
+            send(i, s).wait()
+        return 0
+
+    lax.fori_loop(0, own, drain, 0)
+
+    def drain_half(i, _):
+        for k in (1, 2):
+            keep_half(k, i).wait()
+            for s in (1, 2, 3):
+                send_half(k, i, s).wait()
+        return 0
+
+    lax.fori_loop(0, shared, drain_half, 0)
+
+
+def main_pass(emb, dense, u, ut, logz, w, y, own, shared, groups, peers, tile=TILE, held=2):
     vocab, dim = emb.shape
     toks = u.shape[0]
-    block = vocab // peers
-    tiles = block // tile
     per = tile // LANES
     total = groups * peers
     local = toks // peers
@@ -335,7 +408,7 @@
     hbm = pl.BlockSpec(memory_space=pl.ANY)
     red = 2 * pairs + 2 * groups
     return pl.pallas_call(
-        functools.partial(main_kernel, tile=tile, chunk=chunk, held=held, groups=groups, peers=peers),
+        functools.partial(main_kernel, tile=tile, own=own, shared=shared, held=held, groups=groups, peers=peers),
         in_specs=[hbm, hbm, vmem, vmem, vmem, vmem, vmem],
         out_specs=[hbm, vmem, vmem],
         out_shape=[
@@ -347,7 +420,9 @@
             pltpu.VMEM((2, tile, dim), jnp.bfloat16),
             pltpu.VMEM((2, per, toks, LANES), f32),
             pltpu.VMEM((toks, tile), jnp.bfloat16),
-            pltpu.VMEM((tiles, dim, tile), f32),
+            pltpu.VMEM((2, dim // 2, toks), jnp.bfloat16),
+            pltpu.VMEM((own, dim, tile), f32),
+            pltpu.VMEM((2, shared, dim // 2, tile), f32),
             pltpu.VMEM((toks, dim), f32),
             pltpu.VMEM((8, LANES), f32),
             pltpu.VMEM((pairs, local, dim), f32),
@@ -358,16 +433,19 @@
             pltpu.VMEM((local, dim), f32),
             pltpu.VMEM((total, 16, 128), f32),
             pltpu.SemaphoreType.DMA((2, 2)),
-            pltpu.SemaphoreType.DMA((tiles, peers)),
-            pltpu.SemaphoreType.DMA((tiles, peers)),
-            pltpu.SemaphoreType.DMA((tiles,)),
+            pltpu.SemaphoreType.DMA((own, peers)),
+            pltpu.SemaphoreType.DMA((own, peers)),
+            pltpu.SemaphoreType.DMA((own,)),
+            pltpu.SemaphoreType.DMA((2, shared, 4)),
+            pltpu.SemaphoreType.DMA((2, shared, 4)),
+            pltpu.SemaphoreType.DMA((2, shared)),
             pltpu.SemaphoreType.DMA((red,)),
             pltpu.SemaphoreType.DMA((red,)),
             pltpu.SemaphoreType.DMA((total,)),
             pltpu.SemaphoreType.DMA((total,)),
         ],
         compiler_params=pltpu.CompilerParams(vmem_limit_bytes=63 * MIB, collective_id=0, has_side_effects=True),
-        cost_estimate=pl.CostEstimate(flops=6 * block * dim * toks, bytes_accessed=4 * block * toks, transcendentals=block * toks),
+        cost_estimate=pl.CostEstimate(flops=6 * vocab // peers * dim * toks, bytes_accessed=4 * vocab // peers * toks, transcendentals=vocab // peers * toks),
     )(emb, dense, u, ut, logz, w, y)
 
 
@@ -378,8 +456,6 @@
     def local_head(hidden, embedding, norm_weight, teach_ids, teach_prob, tok_mask):
         vocab_local = embedding.shape[0]
         toks = hidden.shape[0]
-        block = vocab_local // peers
-        high = block // LANES
         dim = hidden.shape[1]
         tp = lax.axis_index('tp')
         dp = lax.axis_index('dp')
@@ -401,10 +477,16 @@
         mask = stats[0, :, 2].reshape(-1, 1)
         weight = mask / jnp.sum(mask)
 
-        base = (tp * vocab_local + dp * block).astype(jnp.int32).reshape(1)
-        dense = teacher_dense(base, ids_all, prob_all, high)
+        tiles = vocab_local // TILE
+        own = OWN
+        shared = tiles // peers - own
+        core, chip = dp % 2, dp // 2
+        starts = [dp * own, peers * own + (2 * (chip // 2) + core) * shared, peers * own + (peers // 2) * shared + (2 * (chip % 2) + core) * shared]
+        base = (jnp.stack(starts) * (TILE // LANES) + tp * (vocab_local // LANES)).astype(jnp.int32)
+        regions = tuple(n * (TILE // LANES) for n in (own, shared, shared))
+        dense = teacher_dense(base, ids_all, prob_all, regions)
         u_all = (normed_all * scale_w).astype(jnp.bfloat16)
-        de_t, grad_u, sums = main_pass(embedding, dense, u_all, u_all.T, log_norm, weight, normed, groups, peers)
+        de_t, grad_u, sums = main_pass(embedding, dense, u_all, u_all.T, log_norm, weight, normed, own, shared, groups, peers)
         used = dim // 128
         grad_norm = sums[:used].reshape(dim)
         loss_mean = jnp.sum(weight * log_norm) - jnp.sum(sums[used])

time: 470 us -> 422 us (0.90)
  Pallas kernels: 406 us -> 358 us
    pallas_call x2, Pallas kernels: 343 us -> 306 us  [the longest x1 209 us: main_pass(): pl.pallas_call(functools.partial(main_kernel, tile=tile, own=own, shared=...]
    pallas_call x1, Pallas kernels: 63.3 us -> 52 us  [local_stats(): pl.pallas_call(functools.partial(stats_kernel, sub=sub, groups=groups, pe...]
  transfers between devices with their start and end apart: 3 -> 3, of which waited for: 0 -> 1; matrix products, arithmetic and copies ran while one was open for 2% -> 2% of each run, Pallas kernels for 31% -> 35%
where the time goes in v3:
time: 422 us; the launch traced here: 421 us
  Pallas kernels  358 us (85%)
  local copies, waits for them, and re-layouts  26.4 us (6%)
  other arithmetic  17.7 us (4%)
  between operations  16.2 us (4%)
    pallas_call x1, Pallas kernels, main_pass(): pl.pallas_call(functools.partial(main_kernel, tile=tile, own=own, shared=...  209 us
    pallas_call x1, Pallas kernels, teacher_dense(): pl.pallas_call(functools.partial(teacher_kernel, regions=regions, group=6...  96.9 us
    pallas_call x1, Pallas kernels, local_stats(): pl.pallas_call(functools.partial(stats_kernel, sub=sub, groups=groups, pe...  52 us
    unnamed x13, local copies, waits for them, and re-layouts  22.2 us
  transfers between devices with their start and end apart: 3, of which 1 were waited for; matrix products, arithmetic and copies ran while one was open for 2% of the time, Pallas kernels for 35%

profile of v3, /device:TPU:0, one launch (start us, length us, event | category | flops | bytes accessed | tf_op | source)
XLA Modules:
  0.0 421.1 jit_solution(16142036098085150449)
XLA Ops:
  7.2 0.0 all-gather.4.cloned.1.call-start
  7.2 0.7 all-gather.4.cloned.1.call-update
  7.9 0.0 all-gather.6.cloned.1.call-start
  7.9 0.7 all-gather.6.cloned.1.call-update
  8.6 0.0 all-gather.8.cloned.1.call-start
  8.7 1.1 fusion
  9.8 0.7 broadcast_add_fusion
  10.5 2.0 convert_multiply_fusion
  12.5 0.0 all-gather.8.cloned.1.call-update
  12.6 0.2 copy.14.ut_ref
  12.7 0.0 copy-start
  12.7 0.7 copy-done
  13.4 52.0 %shard_map.93 = f32[32,8,256]{2,1,0:T(8,128)S(1)} custom-call(bf16[65536,640]{1,0:T(8,128)(2,1)} %emb.1, bf16[640,256]{1,0:T(8,128)(2,1)S(1)} %copy.14.ut_ref, f32[1,256]{1,0:T(1,128)S(1)} %bitcast.41), custom_call_target="tpu_custom_call" | custom-call | flops 21474836480 | bytes 83886080 | tf_op jit(solution)/shard_map/pallas_call | solution.py:90
  65.4 0.1 fusion.11
  65.5 0.6 fusion.10
  66.1 1.2 fusion.8
  67.4 1.4 copy.26
  68.8 1.4 copy.28
  70.1 0.1 fusion.9.base_ref
  70.2 1.5 all-gather.6.cloned.1.call-done.prob_ref
  71.7 1.6 copy-done.1
  73.3 1.6 copy-done.2
  74.9 96.9 %shard_map.94.dense = f32[96,2048,128]{2,1,0:T(8,128)} custom-call(s32[3]{0:T(128)S(1)} %fusion.9.base_ref, s32[2048,256]{1,0:T(8,128)S(1)} %copy-done.1, f32[2048,256]{1,0:T(8,128)S(1)} %copy-done.2), custom_call_target="tpu_custom_call" | custom-call | flops 38654705664 | bytes 100663296 | tf_op jit(solution)/shard_map/pallas_call | solution.py:145
  171.8 2.9 fusion.12
  174.7 2.7 copy.17.ut_ref
  177.4 4.4 %multiply_convert_fusion.u_ref = bf16[2048,640]{1,0:T(8,128)(2,1)} fusion(f32[2048,640]{1,0:T(8,128)} %all-gather.8.cloned.1.call-done, f32[640]{0:T(1024)S(1)} %broadcast_add_fusion), kind=kLoop, calls=%fused_computation | loop fusion | flops 2621440 | bytes 7866880 | tf_op jit(solution)/shard_map/convert_element_type | solution.py:488
  181.8 209.0 %shard_map.95 = (f32[80,65536]{1,0:T(8,128)}, f32[256,640]{1,0:T(8,128)}, f32[16,128]{1,0:T(8,128)}) custom-call(bf16[65536,640]{1,0:T(8,128)(2,1)} %emb.1, f32[96,2048,128]{2,1,0:T(8,128)} %shard_map.94.dense, bf16[2048,640]{1,0:T(8,128)(2,1)} %multiply_convert_fusion.u_ref, bf16[640,2048]{1,0:T(8,128)(2,1)} %copy.17.ut_ref, f32[2048,1]{1,0:T(8,128)} %bitcast.43, ...), custom_call_target="tpu_custom_call" | custom-call | flops 64424509440 | bytes 67108864 | tf_op jit(solution)/shard_map/pallas_call | solution.py:410
  390.8 1.3 slice_reduce_fusion
  392.1 1.3 slice_bitcast_fusion
  393.3 1.3 multiply_reduce_fusion
  394.7 2.0 multiply_convert_fusion.1
  397.9 15.6 %copy.45 = f32[65536,80]{0,1:T(8,128)} copy(f32[65536,80]{0,1:T(8,128)} %bitcast.42) | data formatting | bytes 41943040
  (12 shorter events, 0.1 us)
Async XLA Ops:
  7.2 63.1 %all-gather.4.cloned.1.call-start = ((), (), s32[]{:S(2)}) async-start(), calls=%async_computation | async-start | bytes 2359296 | tf_op jit(solution)/shard_map/all_gather | solution.py:467
  7.9 63.8 %all-gather.6.cloned.1.call-start = ((), (), s32[]{:S(2)}) async-start(), calls=%async_computation.1 | async-start | bytes 2359296 | tf_op jit(solution)/shard_map/all_gather | solution.py:468
  8.6 163.2 %all-gather.8.cloned.1.call-start = ((), (), s32[]{:S(2)}) async-start(), calls=%async_computation.2 | async-start | bytes 5898240 | tf_op jit(solution)/shard_map/all_gather | solution.py:469
  12.7 0.7 copy-start
  71.7 1.6 copy-start.1
  73.3 1.6 copy-start.2
  181.8 211.6 %copy-start.3 = (bf16[256,640]{1,0:T(8,128)(2,1)S(1)}, bf16[256,640]{1,0:T(8,128)(2,1)}, u32[]{:S(2)}) copy-start(bf16[256,640]{1,0:T(8,128)(2,1)} %param.6) | copy-start | bytes 983044
Sparse Core Ops, SparseCore 0:
  9.9 30.2 all-gather.3
  42.1 29.6 all-gather.5
  73.6 39.7 all-gather.7

commit v4 on v3

--- a/solution.py
+++ b/solution.py
@@ -11,6 +11,7 @@
 LANES = 128
 TILE = 512
 OWN = 8
+HELD = 3
 MIB = 1024 * 1024
 NT = (((1,), (1,)), ((), ()))
 MESH = pl.DeviceIdType.MESH
@@ -153,9 +154,9 @@
     )(base, ids, prob)
 
 
-def main_kernel(emb, dense, u_ref, ut_ref, logz_ref, w_ref, y_ref, out, du_full, sums_out,
+def main_kernel(emb, dense, u_ref, ut_ref, logz_ref, w_ref, y_ref, out, g_keep, du_full, sums_out,
                 emb_buf, dense_buf, g_buf, ut_half, de_buf, de_half, du_ref, tsum_ref, core_buf, z_buf, xy_buf, tot_ref, mine_ref, du_out, sums_ref,
-                in_sem, send_sem, recv_sem, own_sem, half_send, half_recv, half_own, red_send, red_recv, all_send, all_recv,
+                in_sem, g_put, g_get, send_sem, recv_sem, own_sem, half_send, half_recv, half_own, red_send, red_recv, all_send, all_recv,
                 *, tile, own, shared, held, groups, peers):
     toks, dim = u_ref.shape
     cols = dim // peers
@@ -232,7 +233,7 @@
         ut_half[0, j * quarter:(j + 1) * quarter, :] = ut_ref[lines, :]
     ut_half[1] = ut_ref[pl.ds(pl.multiple_of(y_pos * wide, 16), wide), :]
 
-    def gradient(rows, slot, counted):
+    def gradient(rows, slot, buf, counted):
         e = emb_buf[slot]
         z = lax.dot_general(u_ref[rows, :], e, NT, preferred_element_type=jnp.float32)
         w = w_ref[rows, :]
@@ -241,12 +242,12 @@
         for h in range(per):
             zh = z[:, h * LANES:(h + 1) * LANES]
             q = dense_buf[slot, h, rows, :] * w
-            g_buf[rows, h * LANES:(h + 1) * LANES] = (jnp.exp(zh - logz) * w - q).astype(jnp.bfloat16)
+            g_buf[buf, rows, h * LANES:(h + 1) * LANES] = (jnp.exp(zh - logz) * w - q).astype(jnp.bfloat16)
             if counted:
                 acc = acc + jnp.sum((q * zh).reshape(chunk // 8, 8, LANES), axis=0)
         if counted:
             tsum_ref[...] += acc
-            du_ref[rows, :] += jnp.dot(g_buf[rows, :], e, preferred_element_type=jnp.float32)
+            du_ref[rows, :] += jnp.dot(g_buf[buf, rows, :], e, preferred_element_type=jnp.float32)
 
     def own_step(i, _):
         slot = lax.rem(i, 2)
@@ -261,11 +262,11 @@
             begin(1, 0, 0)
 
         def part(c, _):
-            gradient(pl.ds(pl.multiple_of(c * chunk, chunk), chunk), slot, True)
+            gradient(pl.ds(pl.multiple_of(c * chunk, chunk), chunk), slot, 0, True)
             return 0
 
         lax.fori_loop(0, 2, part, 0)
-        de_buf[i] = jnp.dot(ut_ref[...], g_buf[...], preferred_element_type=jnp.float32)
+        de_buf[i] = jnp.dot(ut_ref[...], g_buf[0], preferred_element_type=jnp.float32)
         keep(i).start()
         for s in range(peers - 1, 0, -1):
             send(i, s).start()
@@ -277,6 +278,12 @@
         for k in (1, 2):
             for s in (3, 2, 1):
                 send_half(k, i, s).start()
+
+    def store(k, i):
+        return pltpu.make_async_copy(g_buf.at[k - 1], g_keep.at[k - 1, i], g_put.at[k - 1])
+
+    def load(k, i):
+        return pltpu.make_async_copy(g_keep.at[k - 1, i], g_buf.at[k - 1], g_get.at[k - 1])
 
     def shared_step(i, _):
         for k, half in ((1, x_pos), (2, y_pos)):
@@ -288,10 +295,29 @@
                 @pl.when(i + 1 < shared)
                 def _():
                     begin(1, i + 1, 0)
-            gradient(pl.ds(pl.multiple_of((1 - half) * chunk, chunk), chunk), slot, False)
-            gradient(pl.ds(pl.multiple_of(half * chunk, chunk), chunk), slot, True)
-            de_half[k - 1, i] = jnp.dot(ut_half[k - 1], g_buf[...], preferred_element_type=jnp.float32)
+            @pl.when(i > 0)
+            def _():
+                store(k, i - 1).wait()
+
+            gradient(pl.ds(pl.multiple_of((1 - half) * chunk, chunk), chunk), slot, slot, False)
+            gradient(pl.ds(pl.multiple_of(half * chunk, chunk), chunk), slot, slot, True)
+            store(k, i).start()
+        return 0
+
+    lax.fori_loop(0, shared, shared_step, 0)
+    for k in (1, 2):
+        store(k, shared - 1).wait()
+        load(k, 0).start()
+
+    def late_step(i, _):
+        for k in (1, 2):
+            load(k, i).wait()
+            de_half[k - 1, i] = jnp.dot(ut_half[k - 1], g_buf[k - 1], preferred_element_type=jnp.float32)
             keep_half(k, i).start()
+
+            @pl.when(i + 1 < shared)
+            def _():
+                load(k, i + 1).start()
 
         @pl.when(i < shared - held)
         def _():
@@ -299,8 +325,6 @@
 
         return 0
 
-    lax.fori_loop(0, shared, shared_step, 0)
-
     def to_core(q):
         rows = pl.ds(pl.multiple_of((2 * q + (1 - core)) * local, local), local)
         return pltpu.make_async_remote_copy(
@@ -309,6 +333,7 @@
 
     for q in range(pairs):
         to_core(q).start()
+    lax.fori_loop(0, 2, late_step, 0)
     for q in range(pairs):
         to_core(q).wait()
     for q in range(pairs):
@@ -323,6 +348,7 @@
 
     for s in range(1, groups):
         to_z(s).start()
+    lax.fori_loop(2, shared, late_step, 0)
     for s in range(1, groups):
         to_z(s).wait()
     mine = core_buf[:, pl.ds(pl.multiple_of(tp * part_rows, part_rows), part_rows), :]
@@ -396,7 +422,7 @@
     lax.fori_loop(0, shared, drain_half, 0)
 
 
-def main_pass(emb, dense, u, ut, logz, w, y, own, shared, groups, peers, tile=TILE, held=2):
+def main_pass(emb, dense, u, ut, logz, w, y, own, shared, groups, peers, tile=TILE, held=HELD):
     vocab, dim = emb.shape
     toks = u.shape[0]
     per = tile // LANES
@@ -410,16 +436,17 @@
     return pl.pallas_call(
         functools.partial(main_kernel, tile=tile, own=own, shared=shared, held=held, groups=groups, peers=peers),
         in_specs=[hbm, hbm, vmem, vmem, vmem, vmem, vmem],
-        out_specs=[hbm, vmem, vmem],
+        out_specs=[hbm, hbm, vmem, vmem],
         out_shape=[
             jax.ShapeDtypeStruct((dim // peers, vocab), f32),
+            jax.ShapeDtypeStruct((2, shared, toks, tile), jnp.bfloat16),
             jax.ShapeDtypeStruct((local, dim), f32),
             jax.ShapeDtypeStruct((16, 128), f32),
         ],
         scratch_shapes=[
             pltpu.VMEM((2, tile, dim), jnp.bfloat16),
             pltpu.VMEM((2, per, toks, LANES), f32),
-            pltpu.VMEM((toks, tile), jnp.bfloat16),
+            pltpu.VMEM((2, toks, tile), jnp.bfloat16),
             pltpu.VMEM((2, dim // 2, toks), jnp.bfloat16),
             pltpu.VMEM((own, dim, tile), f32),
             pltpu.VMEM((2, shared, dim // 2, tile), f32),
@@ -433,6 +460,8 @@
             pltpu.VMEM((local, dim), f32),
             pltpu.VMEM((total, 16, 128), f32),
             pltpu.SemaphoreType.DMA((2, 2)),
+            pltpu.SemaphoreType.DMA((2,)),
+            pltpu.SemaphoreType.DMA((2,)),
             pltpu.SemaphoreType.DMA((own, peers)),
             pltpu.SemaphoreType.DMA((own, peers)),
             pltpu.SemaphoreType.DMA((own,)),
@@ -486,7 +515,7 @@
         regions = tuple(n * (TILE // LANES) for n in (own, shared, shared))
         dense = teacher_dense(base, ids_all, prob_all, regions)
         u_all = (normed_all * scale_w).astype(jnp.bfloat16)
-        de_t, grad_u, sums = main_pass(embedding, dense, u_all, u_all.T, log_norm, weight, normed, own, shared, groups, peers)
+        de_t, _, grad_u, sums = main_pass(embedding, dense, u_all, u_all.T, log_norm, weight, normed, own, shared, groups, peers)
         used = dim // 128
         grad_norm = sums[:used].reshape(dim)
         loss_mean = jnp.sum(weight * log_norm) - jnp.sum(sums[used])

time: 422 us -> 420 us (level); the launches traced: 421 us -> 414 us
  Pallas kernels: 358 us -> 350 us
    pallas_call x1, Pallas kernels: 209 us -> 202 us  [main_pass(): pl.pallas_call(functools.partial(main_kernel, tile=tile, own=own, shared=...]
  transfers between devices with their start and end apart: 3 -> 3, of which waited for: 1 -> 1; matrix products, arithmetic and copies ran while one was open for 2% -> 2% of each run, Pallas kernels for 35% -> 36%
where the time goes in v4:
time: 420 us; the launch traced here: 414 us
  Pallas kernels  350 us (83%)
  local copies, waits for them, and re-layouts  26.4 us (6%)
  other arithmetic  17.8 us (4%)
  between operations  16.3 us (4%)
    pallas_call x1, Pallas kernels, main_pass(): pl.pallas_call(functools.partial(main_kernel, tile=tile, own=own, shared=...  202 us
    pallas_call x1, Pallas kernels, teacher_dense(): pl.pallas_call(functools.partial(teacher_kernel, regions=regions, group=6...  96.9 us
    pallas_call x1, Pallas kernels, local_stats(): pl.pallas_call(functools.partial(stats_kernel, sub=sub, groups=groups, pe...  52 us
    unnamed x13, local copies, waits for them, and re-layouts  22.2 us
  transfers between devices with their start and end apart: 3, of which 1 were waited for; matrix products, arithmetic and copies ran while one was open for 2% of the time, Pallas kernels for 36%

profile of v4, /device:TPU:0, one launch (start us, length us, event | category | flops | bytes accessed | tf_op | source)
XLA Modules:
  0.0 413.9 jit_solution(7495324535425550102)
XLA Ops:
  7.2 0.0 all-gather.4.cloned.1.call-start
  7.2 0.7 all-gather.4.cloned.1.call-update
  7.9 0.0 all-gather.6.cloned.1.call-start
  7.9 0.7 all-gather.6.cloned.1.call-update
  8.6 0.0 all-gather.8.cloned.1.call-start
  8.7 1.1 fusion
  9.8 0.7 broadcast_add_fusion
  10.5 2.0 convert_multiply_fusion
  12.5 0.0 all-gather.8.cloned.1.call-update
  12.6 0.2 copy.14.ut_ref
  12.8 0.0 copy-start
  12.8 0.7 copy-done
  13.5 52.0 %shard_map.93 = f32[32,8,256]{2,1,0:T(8,128)S(1)} custom-call(bf16[65536,640]{1,0:T(8,128)(2,1)} %emb.1, bf16[640,256]{1,0:T(8,128)(2,1)S(1)} %copy.14.ut_ref, f32[1,256]{1,0:T(1,128)S(1)} %bitcast.41), custom_call_target="tpu_custom_call" | custom-call | flops 21474836480 | bytes 83886080 | tf_op jit(solution)/shard_map/pallas_call | solution.py:91
  65.5 0.1 fusion.11
  65.6 0.6 fusion.10
  66.2 1.3 fusion.8
  67.5 1.3 copy.26
  68.8 1.4 copy.28
  70.3 0.1 fusion.9.base_ref
  70.4 1.5 all-gather.6.cloned.1.call-done.prob_ref
  71.8 1.6 copy-done.1
  73.4 1.6 copy-done.2
  75.0 96.9 %shard_map.94.dense = f32[96,2048,128]{2,1,0:T(8,128)} custom-call(s32[3]{0:T(128)S(1)} %fusion.9.base_ref, s32[2048,256]{1,0:T(8,128)S(1)} %copy-done.1, f32[2048,256]{1,0:T(8,128)S(1)} %copy-done.2), custom_call_target="tpu_custom_call" | custom-call | flops 38654705664 | bytes 100663296 | tf_op jit(solution)/shard_map/pallas_call | solution.py:146
  171.9 2.9 fusion.12
  174.8 2.8 copy.17.ut_ref
  177.5 4.4 %multiply_convert_fusion.u_ref = bf16[2048,640]{1,0:T(8,128)(2,1)} fusion(f32[2048,640]{1,0:T(8,128)} %all-gather.8.cloned.1.call-done, f32[640]{0:T(1024)S(1)} %broadcast_add_fusion), kind=kLoop, calls=%fused_computation | loop fusion | flops 2621440 | bytes 7866880 | tf_op jit(solution)/shard_map/convert_element_type | solution.py:517
  181.9 201.5 %shard_map.95 = (f32[80,65536]{1,0:T(8,128)}, bf16[2,8,2048,512]{3,2,1,0:T(8,128)(2,1)}, f32[256,640]{1,0:T(8,128)}, f32[16,128]{1,0:T(8,128)}) custom-call(bf16[65536,640]{1,0:T(8,128)(2,1)} %emb.1, f32[96,2048,128]{2,1,0:T(8,128)} %shard_map.94.dense, bf16[2048,640]{1,0:T(8,128)(2,1)} %multiply_convert_fusion.u_ref, bf16[640,2048]{1,0:T(8,128)(2,1)} %copy.17.ut_ref, ...), custom_call_target="tpu_custom_call" | custom-call | flops 64424509440 | bytes 67108864 | tf_op jit(solution)/shard_map/pallas_call | solution.py:436
  383.5 1.3 slice_reduce_fusion
  384.8 1.3 slice_bitcast_fusion
  386.0 1.3 multiply_reduce_fusion
  387.4 2.0 multiply_convert_fusion.1
  390.7 15.6 %copy.45 = f32[65536,80]{0,1:T(8,128)} copy(f32[65536,80]{0,1:T(8,128)} %bitcast.42) | data formatting | bytes 41943040
  (12 shorter events, 0.1 us)
Async XLA Ops:
  7.2 63.2 %all-gather.4.cloned.1.call-start = ((), (), s32[]{:S(2)}) async-start(), calls=%async_computation | async-start | bytes 2359296 | tf_op jit(solution)/shard_map/all_gather | solution.py:496
  7.9 63.9 %all-gather.6.cloned.1.call-start = ((), (), s32[]{:S(2)}) async-start(), calls=%async_computation.1 | async-start | bytes 2359296 | tf_op jit(solution)/shard_map/all_gather | solution.py:497
  8.6 163.3 %all-gather.8.cloned.1.call-start = ((), (), s32[]{:S(2)}) async-start(), calls=%async_computation.2 | async-start | bytes 5898240 | tf_op jit(solution)/shard_map/all_gather | solution.py:498
  12.8 0.7 copy-start
  71.8 1.6 copy-start.1
  73.4 1.6 copy-start.2
  181.9 204.1 %copy-start.3 = (bf16[256,640]{1,0:T(8,128)(2,1)S(1)}, bf16[256,640]{1,0:T(8,128)(2,1)}, u32[]{:S(2)}) copy-start(bf16[256,640]{1,0:T(8,128)(2,1)} %param.6) | copy-start | bytes 983044
Sparse Core Ops, SparseCore 0:
  9.9 30.2 all-gather.3
  42.0 29.7 all-gather.5
  73.7 39.6 all-gather.7
